TPU v7x, 32 devices: a whole 2x2x4 slice. The times are simulated.
32 devices in a mesh: gx: 4 (over y, x), gy: 2 (over core), gz: 4 (over z).
Axes of the slice: x: 2, y: 2, z: 4, core: 2. Of those that a mesh axis runs over, the one named last changes fastest.
Arguments:
- dual_operators: bfloat16 [4, 2, 4, 768, 768], P('gx', 'gy', 'gz'), may hold values from -1 to 3, as said below
- dual_load: float32 [4, 2, 4, 32, 384], P('gx', 'gy', 'gz'), may hold values from -25 to 25
- rigid_modes: float32 [4, 2, 4, 6, 768], P('gx', 'gy', 'gz'), may hold values from -0.21875 to 0.21875
- coarse_load: float32 [4, 2, 4, 6, 32], P('gx', 'gy', 'gz'), may hold values from -24 to 24
- mode_counts: int32 [4, 2, 4], P('gx', 'gy', 'gz'), may hold values from 3 to 6
- face_maps: int32 [4, 2, 4, 3, 128], P('gx', 'gy', 'gz'), may hold values from 0 to 127, each once within a row
Outputs:
- multipliers: float32 [4, 2, 4, 32, 384], P('gx', 'gy', 'gz')
- residual: float32 [4, 2, 4, 32, 384], P('gx', 'gy', 'gz')
Inputs may be any that keep to these rules, and one draw needn't show every extreme that they name: Each dual_operators[i, j, k] is symmetric positive definite. Subdomain s uses rows 0 to mode_counts[s] - 1 of rigid_modes[s]. Each face_maps[i, j, k, d] holds every number of 0 to 127 once.
All inputs are finite; a program needn't handle non-finite values.
Results may differ from a plain program's by a relative error of at most 0.012.
Values sent between devices are 32-bit elements; how exact they have to be, the bound alone decides.
A program may use at most 64 MiB of HBM per device.

v0:
```python
import jax
import jax.numpy as jnp
from jax import lax
from jax.sharding import PartitionSpec as P

ITERS = 2


def extended(array, sides, width):
    for axis, dim in sides:
        size, length = (lax.axis_size(axis), array.shape[dim])
        up = [(i, (i + 1) % size) for i in range(size - 1)]
        down = [(j, i) for i, j in up]
        last = lax.slice_in_dim(array, length - width, length, axis=dim)
        leading = lax.slice_in_dim(array, 0, width, axis=dim)
        before = lax.ppermute(last, axis, up)
        after = lax.ppermute(leading, axis, down)
        array = jnp.concatenate([before, array, after], axis=dim)
    return array


def forward_order(values, permuter):
    return jnp.einsum("xyzrk,xyzkj->xyzrj", values, permuter, precision=lax.Precision.HIGHEST)


def backward_order(values, permuter):
    return jnp.einsum("xyzrk,xyzjk->xyzrj", values, permuter, precision=lax.Precision.HIGHEST)


def side_flags(position, extent):
    return jnp.stack([position > 0, position < extent - 1], axis=-1).astype(jnp.float32)


def interface_mask(first_flags, second_flags, third_flags, face_width):
    present = jnp.concatenate(
        [
            first_flags[:, None, None, :],
            second_flags[None, :, None, :],
            third_flags[None, None, :, :],
        ],
        axis=-1,
    )
    return jnp.repeat(present, face_width, axis=-1)[:, :, :, None, :]


def face_block(values, face_index, face_width):
    return values[..., face_index * face_width : (face_index + 1) * face_width]


def edge_pair(lower_part, upper_part, spatial):
    length = upper_part.shape[spatial]
    lowest = lax.slice_in_dim(lower_part, 0, 1, axis=spatial)
    highest = lax.slice_in_dim(upper_part, length - 1, length, axis=spatial)
    return jnp.concatenate([lowest, highest], axis=spatial)


def neighbour_faces(lower_part, upper_part, received, spatial):
    length = upper_part.shape[spatial]
    from_below = jnp.concatenate(
        [
            lax.slice_in_dim(received, 0, 1, axis=spatial),
            lax.slice_in_dim(upper_part, 0, length - 1, axis=spatial),
        ],
        axis=spatial,
    )
    from_above = jnp.concatenate(
        [
            lax.slice_in_dim(lower_part, 1, length, axis=spatial),
            lax.slice_in_dim(received, 3, 4, axis=spatial),
        ],
        axis=spatial,
    )
    return (from_below, from_above)


def face_halos(edge_pairs):
    first_side = extended(edge_pairs[0], (("gx", 0),), 1)
    second_side = extended(edge_pairs[1], (("gy", 1),), 1)
    third_side = extended(edge_pairs[2], (("gz", 2),), 1)
    return (first_side, second_side, third_side)


def assemble(local_values, permuters, present, face_width):
    minus_faces = [face_block(local_values, 2 * spatial, face_width) for spatial in range(3)]
    plus_faces = [face_block(local_values, 2 * spatial + 1, face_width) for spatial in range(3)]
    owner_minus = [backward_order(minus_faces[spatial], permuters[spatial]) for spatial in range(3)]
    received_all = face_halos(
        [edge_pair(owner_minus[spatial], plus_faces[spatial], spatial) for spatial in range(3)]
    )
    pieces = []
    for spatial in range(3):
        from_below, from_above = neighbour_faces(
            owner_minus[spatial], plus_faces[spatial], received_all[spatial], spatial
        )
        pieces.append(minus_faces[spatial] - forward_order(from_below, permuters[spatial]))
        pieces.append(plus_faces[spatial] - from_above)
    return jnp.concatenate(pieces, axis=-1) * present


def spread_coarse(coefficients, mode_rows):
    return jnp.einsum(
        "xyzmr,xyzmi->xyzri", coefficients, mode_rows, precision=lax.Precision.HIGHEST
    )


def coarse_factor(mode_rows, active):
    identity = jnp.eye(active.shape[-1], dtype=jnp.float32)
    normal_matrix = jnp.einsum(
        "xyzmi,xyzni->xyzmn", mode_rows, mode_rows, precision=lax.Precision.HIGHEST
    )
    normal_matrix = normal_matrix + identity * (1.0 - active)[..., None, :]
    factor = jnp.linalg.cholesky(normal_matrix)
    return jax.scipy.linalg.cho_solve(
        (factor, True), jnp.broadcast_to(identity, normal_matrix.shape)
    )


def owned_faces(values, face_width):
    return jnp.concatenate(
        [
            face_block(values, 1, face_width),
            face_block(values, 3, face_width),
            face_block(values, 5, face_width),
        ],
        axis=-1,
    )


def pairing(first_vectors, second_vectors, face_width):
    return jnp.einsum(
        "xyzri,xyzsi->rs",
        owned_faces(first_vectors, face_width),
        owned_faces(second_vectors, face_width),
        precision=lax.Precision.HIGHEST,
    )


def combine_columns(vectors, matrix):
    return jnp.einsum("xyzri,rs->xyzsi", vectors, matrix, precision=lax.Precision.HIGHEST)


def cholesky_solve(matrix, right_side):
    factor = jnp.linalg.cholesky(matrix)
    return jax.scipy.linalg.cho_solve((factor, True), right_side)


def local(dual_operators, dual_load, rigid_modes, coarse_load, mode_counts, face_maps):
    along_first = dual_load.shape[0]
    along_second = dual_load.shape[1]
    along_third = dual_load.shape[2]
    face_width = dual_load.shape[4] // 3
    mode_total = rigid_modes.shape[3]
    first_flags = side_flags(
        lax.axis_index("gx") * along_first + jnp.arange(along_first),
        along_first * lax.axis_size("gx"),
    )
    second_flags = side_flags(
        lax.axis_index("gy") * along_second + jnp.arange(along_second),
        along_second * lax.axis_size("gy"),
    )
    third_flags = side_flags(
        lax.axis_index("gz") * along_third + jnp.arange(along_third),
        along_third * lax.axis_size("gz"),
    )
    present = interface_mask(first_flags, second_flags, third_flags, face_width)
    positions = jnp.arange(face_width, dtype=jnp.int32)
    permuters = [
        (face_maps[:, :, :, spatial, None, :] == positions[:, None]).astype(jnp.float32)
        for spatial in range(3)
    ]
    active = (jnp.arange(mode_total)[None, None, None, :] < mode_counts[..., None]).astype(
        jnp.float32
    )
    mode_rows = rigid_modes * present * active[..., None]
    coarse_inverse = coarse_factor(mode_rows, active)

    def coarse_field(coefficients):
        return assemble(spread_coarse(coefficients, mode_rows), permuters, present, face_width)

    def precondition(current):
        weights = jnp.einsum(
            "xyzmi,xyzri->xyzmr", mode_rows, current, precision=lax.Precision.HIGHEST
        )
        coefficients = jnp.einsum(
            "xyzmn,xyznr->xyzmr", coarse_inverse, weights, precision=lax.Precision.HIGHEST
        )
        return current - 0.25 * coarse_field(coefficients)

    def operator(current):
        products = jnp.einsum(
            "xyzrk,xyzki->xyzri",
            current.astype(jnp.bfloat16),
            dual_operators,
            preferred_element_type=jnp.float32,
        )
        return assemble(products, permuters, present, face_width)

    empty_face = jnp.zeros_like(dual_load[..., :face_width])
    spread_load = jnp.concatenate(
        [
            empty_face,
            dual_load[..., :face_width],
            empty_face,
            dual_load[..., face_width : 2 * face_width],
            empty_face,
            dual_load[..., 2 * face_width :],
        ],
        axis=-1,
    )
    right_local = assemble(spread_load, permuters, present, face_width)
    initial = coarse_field(
        jnp.einsum(
            "xyzmn,xyznr->xyzmr",
            coarse_inverse,
            coarse_load * active[..., None],
            precision=lax.Precision.HIGHEST,
        )
    )
    residual = right_local - operator(initial)
    projected = precondition(residual)
    projected_image = operator(projected)
    residual_gram, direction_gram = lax.psum(
        (pairing(projected, residual, face_width), pairing(projected, projected_image, face_width)),
        ("gx", "gy", "gz"),
    )
    direction = projected
    image = projected_image
    step_gram = cholesky_solve(direction_gram, residual_gram)
    multipliers = initial + combine_columns(direction, step_gram)
    residual = residual - combine_columns(image, step_gram)

    def iterate(iteration, state_tuple):
        multipliers, residual, direction, image, residual_gram, direction_gram = state_tuple
        projected = precondition(residual)
        projected_image = operator(projected)
        fresh_gram, image_gram, cross_gram, return_gram = lax.psum(
            (
                pairing(projected, residual, face_width),
                pairing(projected, projected_image, face_width),
                pairing(projected, image, face_width),
                pairing(direction, projected_image, face_width),
            ),
            ("gx", "gy", "gz"),
        )
        update_gram = cholesky_solve(residual_gram, fresh_gram)
        carried = jnp.dot(cross_gram, update_gram, precision=lax.Precision.HIGHEST)
        returned = jnp.dot(update_gram.T, return_gram, precision=lax.Precision.HIGHEST)
        kept = jnp.dot(
            update_gram.T,
            jnp.dot(direction_gram, update_gram, precision=lax.Precision.HIGHEST),
            precision=lax.Precision.HIGHEST,
        )
        direction_gram = image_gram + carried + returned + kept
        direction = projected + combine_columns(direction, update_gram)
        image = projected_image + combine_columns(image, update_gram)
        step_gram = cholesky_solve(direction_gram, fresh_gram)
        multipliers = multipliers + combine_columns(direction, step_gram)
        residual = residual - combine_columns(image, step_gram)
        return (multipliers, residual, direction, image, fresh_gram, direction_gram)

    final_state = lax.fori_loop(
        1, ITERS, iterate, (multipliers, residual, direction, image, residual_gram, direction_gram)
    )
    return (owned_faces(final_state[0], face_width), owned_faces(final_state[1], face_width))


def solution(mesh):
    return jax.shard_map(
        local,
        mesh=mesh,
        in_specs=(
            P("gx", "gy", "gz", None, None),
            P("gx", "gy", "gz", None, None),
            P("gx", "gy", "gz", None, None),
            P("gx", "gy", "gz", None, None),
            P("gx", "gy", "gz"),
            P("gx", "gy", "gz", None, None),
        ),
        out_specs=(P("gx", "gy", "gz", None, None), P("gx", "gy", "gz", None, None)),
        check_vma=False,
    )
```

profile of v0, /device:TPU:0, one launch (start us, length us, event | category | flops | bytes accessed | tf_op | source)
XLA Modules:
  0.0 264.5 jit_solution(14579438085977279640)
XLA Ops:
  1.5 4.9 %collective-permute-start.6 = (f32[1,1,1,32,128]{4,3,2,1,0:T(8,128)S(1)}, f32[1,1,1,32,128]{4,3,2,1,0:T(8,128)S(1)}, u32[]{:S(2)}, u32[]{:S(2)}) collective-permute-start(f32[1,1,1,32,128]{4,3,2,1,0:T(8,128)S(1)} %slice.282), channel_id=1, source_target_pairs={{0,8},{8,16},{16,24},{1,9},{9,17},{17,25},{2,10},{10,18},{18,26},{... | collective-permute-start | bytes 49160 | tf_op jit(solution)/shard_map/ppermute | solution.py:16
  7.2 1.3 collective-permute-start.9
  8.6 1.3 collective-permute-start.7
  10.1 1.3 collective-permute-start.11
  17.3 4.5 %collective-permute-start = (f32[1,1,1,32,128]{4,3,2,1,0:T(8,128)S(1)}, f32[1,1,1,32,128]{4,3,2,1,0:T(8,128)S(1)}, u32[]{:S(2)}, u32[]{:S(2)}) collective-permute-start(f32[1,1,1,32,128]{4,3,2,1,0:T(8,128)S(1)} %get-tuple-element.96), channel_id=1, source_target_pairs={{0,8},{8,16},{16,24},{1,9},{9,17},{17,25},{2,10},{10,18},{18,26},{... | collective-permute-start | bytes 49160 | tf_op jit(solution)/shard_map/ppermute | solution.py:16
  24.7 4.6 %collective-permute-done.1 = f32[1,1,1,32,128]{4,3,2,1,0:T(8,128)S(1)} collective-permute-done((f32[1,1,1,32,128]{4,3,2,1,0:T(8,128)S(1)}, f32[1,1,1,32,128]{4,3,2,1,0:T(8,128)S(1)}, u32[]{:S(2)}, u32[]{:S(2)}) %collective-permute-start.1) | collective-permute-done | bytes 16416 | tf_op jit(solution)/shard_map/ppermute | solution.py:17
  32.8 1.6 collective-permute-done.3
  34.5 4.5 %collective-permute-start.4 = (f32[1,1,1,32,128]{4,3,2,1,0:T(8,128)S(1)}, f32[1,1,1,32,128]{4,3,2,1,0:T(8,128)S(1)}, u32[]{:S(2)}, u32[]{:S(2)}) collective-permute-start(f32[1,1,1,32,128]{4,3,2,1,0:T(8,128)S(1)} %get-tuple-element.94), channel_id=1, source_target_pairs={{0,1},{1,2},{2,3},{4,5},{5,6},{6,7},{8,9},{9,10},{10,11},{12,13},{... | collective-permute-start | bytes 49160 | tf_op jit(solution)/shard_map/ppermute | solution.py:16
  39.0 1.4 collective-permute-done.4
  41.9 4.5 %collective-permute-done.5 = f32[1,1,1,32,128]{4,3,2,1,0:T(8,128)S(1)} collective-permute-done((f32[1,1,1,32,128]{4,3,2,1,0:T(8,128)S(1)}, f32[1,1,1,32,128]{4,3,2,1,0:T(8,128)S(1)}, u32[]{:S(2)}, u32[]{:S(2)}) %collective-permute-start.5) | collective-permute-done | bytes 16416 | tf_op jit(solution)/shard_map/ppermute | solution.py:17
  47.0 5.1 %collective-permute-start.12 = (f32[1,1,1,32,128]{4,3,2,1,0:T(8,128)S(1)}, f32[1,1,1,32,128]{4,3,2,1,0:T(8,128)S(1)}, u32[]{:S(2)}, u32[]{:S(2)}) collective-permute-start(f32[1,1,1,32,128]{4,3,2,1,0:T(8,128)S(1)} %slice.346), channel_id=1, source_target_pairs={{0,8},{8,16},{16,24},{1,9},{9,17},{17,25},{2,10},{10,18},{18,26},{... | collective-permute-start | bytes 49160 | tf_op jit(solution)/shard_map/ppermute | solution.py:16
  52.2 1.3 collective-permute-start.17
  53.8 1.3 collective-permute-start.15
  55.2 1.3 collective-permute-start.13
  56.6 4.2 %collective-permute-done.13 = f32[1,1,1,32,128]{4,3,2,1,0:T(8,128)S(1)} collective-permute-done((f32[1,1,1,32,128]{4,3,2,1,0:T(8,128)S(1)}, f32[1,1,1,32,128]{4,3,2,1,0:T(8,128)S(1)}, u32[]{:S(2)}, u32[]{:S(2)}) %collective-permute-start.13) | collective-permute-done | bytes 16416 | tf_op jit(solution)/shard_map/ppermute | solution.py:17
  60.8 2.1 collective-permute-start.8
  63.8 2.2 collective-permute-start.14
  66.2 4.5 %collective-permute-start.10 = (f32[1,1,1,32,128]{4,3,2,1,0:T(8,128)S(1)}, f32[1,1,1,32,128]{4,3,2,1,0:T(8,128)S(1)}, u32[]{:S(2)}, u32[]{:S(2)}) collective-permute-start(f32[1,1,1,32,128]{4,3,2,1,0:T(8,128)S(1)} %get-tuple-element.98), channel_id=1, source_target_pairs={{0,1},{1,2},{2,3},{4,5},{5,6},{6,7},{8,9},{9,10},{10,11},{12,13},{... | collective-permute-start | bytes 49160 | tf_op jit(solution)/shard_map/ppermute | solution.py:16
  71.0 3.9 %collective-permute-start.16 = (f32[1,1,1,32,128]{4,3,2,1,0:T(8,128)S(1)}, f32[1,1,1,32,128]{4,3,2,1,0:T(8,128)S(1)}, u32[]{:S(2)}, u32[]{:S(2)}) collective-permute-start(f32[1,1,1,32,128]{4,3,2,1,0:T(8,128)S(1)} %get-tuple-element.88), channel_id=1, source_target_pairs={{0,1},{1,2},{2,3},{4,5},{5,6},{6,7},{8,9},{9,10},{10,11},{12,13},{... | collective-permute-start | bytes 49160 | tf_op jit(solution)/shard_map/ppermute | solution.py:16
  77.7 4.7 %collective-permute-start.18 = (f32[1,1,1,32,128]{4,3,2,1,0:T(8,128)S(1)}, f32[1,1,1,32,128]{4,3,2,1,0:T(8,128)S(1)}, u32[]{:S(2)}, u32[]{:S(2)}) collective-permute-start(f32[1,1,1,32,128]{4,3,2,1,0:T(8,128)S(1)} %slice.352), channel_id=1, source_target_pairs={{0,8},{8,16},{16,24},{1,9},{9,17},{17,25},{2,10},{10,18},{18,26},{... | collective-permute-start | bytes 49160 | tf_op jit(solution)/shard_map/ppermute | solution.py:16
  82.5 1.3 collective-permute-start.23
  83.8 1.3 collective-permute-start.21
  85.1 1.3 collective-permute-start.19
  86.5 4.2 %collective-permute-done.19 = f32[1,1,1,32,128]{4,3,2,1,0:T(8,128)S(1)} collective-permute-done((f32[1,1,1,32,128]{4,3,2,1,0:T(8,128)S(1)}, f32[1,1,1,32,128]{4,3,2,1,0:T(8,128)S(1)}, u32[]{:S(2)}, u32[]{:S(2)}) %collective-permute-start.19) | collective-permute-done | bytes 16416 | tf_op jit(solution)/shard_map/ppermute | solution.py:17
  90.7 4.8 %collective-permute-start.22 = (f32[1,1,1,32,128]{4,3,2,1,0:T(8,128)S(1)}, f32[1,1,1,32,128]{4,3,2,1,0:T(8,128)S(1)}, u32[]{:S(2)}, u32[]{:S(2)}) collective-permute-start(f32[1,1,1,32,128]{4,3,2,1,0:T(8,128)S(1)} %get-tuple-element.91), channel_id=1, source_target_pairs={{0,1},{1,2},{2,3},{4,5},{5,6},{6,7},{8,9},{9,10},{10,11},{12,13},{... | collective-permute-start | bytes 49160 | tf_op jit(solution)/shard_map/ppermute | solution.py:16
  95.5 1.7 collective-permute-start.20
  99.4 2.8 %collective-permute-start.24 = (f32[1,1,1,32,128]{4,3,2,1,0:T(8,128)S(1)}, f32[1,1,1,32,128]{4,3,2,1,0:T(8,128)S(1)}, u32[]{:S(2)}, u32[]{:S(2)}) collective-permute-start(f32[1,1,1,32,128]{4,3,2,1,0:T(8,128)S(1)} %slice.361), channel_id=1, source_target_pairs={{0,8},{8,16},{16,24},{1,9},{9,17},{17,25},{2,10},{10,18},{18,26},{... | collective-permute-start | bytes 49160 | tf_op jit(solution)/shard_map/ppermute | solution.py:16
  102.3 1.3 collective-permute-start.29
  103.6 1.3 collective-permute-start.27
  106.3 4.2 %collective-permute-done.25 = f32[1,1,1,32,128]{4,3,2,1,0:T(8,128)S(1)} collective-permute-done((f32[1,1,1,32,128]{4,3,2,1,0:T(8,128)S(1)}, f32[1,1,1,32,128]{4,3,2,1,0:T(8,128)S(1)}, u32[]{:S(2)}, u32[]{:S(2)}) %collective-permute-start.25) | collective-permute-done | bytes 16416 | tf_op jit(solution)/shard_map/ppermute | solution.py:17
  110.5 4.5 %collective-permute-start.28 = (f32[1,1,1,32,128]{4,3,2,1,0:T(8,128)S(1)}, f32[1,1,1,32,128]{4,3,2,1,0:T(8,128)S(1)}, u32[]{:S(2)}, u32[]{:S(2)}) collective-permute-start(f32[1,1,1,32,128]{4,3,2,1,0:T(8,128)S(1)} %get-tuple-element.78), channel_id=1, source_target_pairs={{0,1},{1,2},{2,3},{4,5},{5,6},{6,7},{8,9},{9,10},{10,11},{12,13},{... | collective-permute-start | bytes 49160 | tf_op jit(solution)/shard_map/ppermute | solution.py:16
  115.1 1.7 collective-permute-start.26
  118.5 40.1 %all-reduce.1 = (f32[32,32]{0,1:T(8,128)S(1)}, f32[32,32]{0,1:T(8,128)S(1)}) all-reduce(f32[32,32]{0,1:T(8,128)S(1)} %fusion.54, f32[32,32]{0,1:T(8,128)S(1)} %fusion.73), channel_id=1, replica_groups=mesh['gx'=4,'gy'=2,'gz'=4] {'gx','gy','gz'}, use_global_device_ids=true, to_apply=%region_5.7 | all-reduce | flops 2048 | bytes 16384 | tf_op jit(solution)/shard_map/psum | solution.py:222
  158.7 2.9 %cholesky.92 = f32[32,32]{1,0:T(8,128)S(1)} custom-call(f32[32,32]{1,0:T(8,128)S(1)} %fusion.159), custom_call_target="Cholesky" | custom-call | tf_op jit(solution)/shard_map/jit(cholesky)/cholesky | solution.py:143
  163.0 2.4 custom-call.22
  167.2 2.9 %cholesky.103 = f32[32,32]{1,0:T(8,128)S(1)} custom-call(f32[32,32]{1,0:T(8,128)S(1)} %fusion.142), custom_call_target="Cholesky" | custom-call | tf_op jit(solution)/shard_map/while/body/eval_jaxpr/jit(cholesky)/cholesky | solution.py:143
  171.5 4.2 %collective-permute-start.30 = (f32[1,1,1,32,128]{4,3,2,1,0:T(8,128)S(1)}, f32[1,1,1,32,128]{4,3,2,1,0:T(8,128)S(1)}, u32[]{:S(2)}, u32[]{:S(2)}) collective-permute-start(f32[1,1,1,32,128]{4,3,2,1,0:T(8,128)S(1)} %get-tuple-element.71), channel_id=1, source_target_pairs={{0,8},{8,16},{16,24},{1,9},{9,17},{17,25},{2,10},{10,18},{18,26},{... | collective-permute-start | bytes 49160 | tf_op jit(solution)/shard_map/while/body/eval_jaxpr/ppermute | solution.py:16
  175.8 2.5 custom-call.23
  178.3 1.3 collective-permute-start.35
  182.2 4.5 %collective-permute-start.34 = (f32[1,1,1,32,128]{4,3,2,1,0:T(8,128)S(1)}, f32[1,1,1,32,128]{4,3,2,1,0:T(8,128)S(1)}, u32[]{:S(2)}, u32[]{:S(2)}) collective-permute-start(f32[1,1,1,32,128]{4,3,2,1,0:T(8,128)S(1)} %get-tuple-element.69), channel_id=1, source_target_pairs={{0,1},{1,2},{2,3},{4,5},{5,6},{6,7},{8,9},{9,10},{10,11},{12,13},{... | collective-permute-start | bytes 49160 | tf_op jit(solution)/shard_map/while/body/eval_jaxpr/ppermute | solution.py:16
  186.8 2.7 %collective-permute-start.32 = (f32[1,1,1,32,128]{4,3,2,1,0:T(8,128)S(1)}, f32[1,1,1,32,128]{4,3,2,1,0:T(8,128)S(1)}, u32[]{:S(2)}, u32[]{:S(2)}) collective-permute-start(f32[1,1,1,32,128]{4,3,2,1,0:T(8,128)S(1)} %get-tuple-element.70), channel_id=1, source_target_pairs={{0,4},{1,5},{2,6},{3,7},{8,12},{9,13},{10,14},{11,15},{16,20},{17,... | collective-permute-start | bytes 49160 | tf_op jit(solution)/shard_map/while/body/eval_jaxpr/ppermute | solution.py:16
  191.7 4.3 %collective-permute-start.36 = (f32[1,1,1,32,128]{4,3,2,1,0:T(8,128)S(1)}, f32[1,1,1,32,128]{4,3,2,1,0:T(8,128)S(1)}, u32[]{:S(2)}, u32[]{:S(2)}) collective-permute-start(f32[1,1,1,32,128]{4,3,2,1,0:T(8,128)S(1)} %slice.382), channel_id=1, source_target_pairs={{0,8},{8,16},{16,24},{1,9},{9,17},{17,25},{2,10},{10,18},{18,26},{... | collective-permute-start | bytes 49160 | tf_op jit(solution)/shard_map/while/body/eval_jaxpr/ppermute | solution.py:16
  200.4 4.2 %collective-permute-done.37 = f32[1,1,1,32,128]{4,3,2,1,0:T(8,128)S(1)} collective-permute-done((f32[1,1,1,32,128]{4,3,2,1,0:T(8,128)S(1)}, f32[1,1,1,32,128]{4,3,2,1,0:T(8,128)S(1)}, u32[]{:S(2)}, u32[]{:S(2)}) %collective-permute-start.37) | collective-permute-done | bytes 16416 | tf_op jit(solution)/shard_map/while/body/eval_jaxpr/ppermute | solution.py:17
  204.6 4.5 %collective-permute-start.40 = (f32[1,1,1,32,128]{4,3,2,1,0:T(8,128)S(1)}, f32[1,1,1,32,128]{4,3,2,1,0:T(8,128)S(1)}, u32[]{:S(2)}, u32[]{:S(2)}) collective-permute-start(f32[1,1,1,32,128]{4,3,2,1,0:T(8,128)S(1)} %get-tuple-element.63), channel_id=1, source_target_pairs={{0,1},{1,2},{2,3},{4,5},{5,6},{6,7},{8,9},{9,10},{10,11},{12,13},{... | collective-permute-start | bytes 49160 | tf_op jit(solution)/shard_map/while/body/eval_jaxpr/ppermute | solution.py:16
  209.1 1.9 collective-permute-start.38
  212.6 40.7 %all-reduce = (f32[32,32]{1,0:T(8,128)S(1)}, f32[32,32]{0,1:T(8,128)S(1)}, f32[32,32]{1,0:T(8,128)S(1)}, f32[32,32]{1,0:T(8,128)S(1)}) all-reduce(f32[32,32]{1,0:T(8,128)S(1)} %fusion.59, f32[32,32]{0,1:T(8,128)S(1)} %fusion.71, f32[32,32]{1,0:T(8,128)S(1)} %fusion.72, ...), channel_id=1, replica_groups=mesh['gx'=4,'gy'=2,'gz'=4] {'gx','gy','gz'}, use_global_device_ids=true, to_apply=%region_8.11 | all-reduce | flops 4096 | bytes 32768 | tf_op jit(solution)/shard_map/while/body/eval_jaxpr/psum | solution.py:236
  255.2 2.9 %cholesky.114 = f32[32,32]{1,0:T(8,128)S(1)} custom-call(f32[32,32]{1,0:T(8,128)S(1)} %fusion.137), custom_call_target="Cholesky" | custom-call | tf_op jit(solution)/shard_map/while/body/eval_jaxpr/jit(cholesky)/cholesky | solution.py:143
  259.4 2.4 custom-call.24
  (227 shorter events, 45.9 us)
Async XLA Ops:
  0.6 45.7 %copy-start = (bf16[1,1,1,768,768]{4,3,2,1,0:T(8,128)(2,1)S(1)}, bf16[1,1,1,768,768]{4,3,2,1,0:T(8,128)(2,1)}, u32[]{:S(2)}) copy-start(bf16[1,1,1,768,768]{4,3,2,1,0:T(8,128)(2,1)} %param.9) | copy-start | bytes 3538948
  1.5 50.7 %collective-permute-start.6 = (f32[1,1,1,32,128]{4,3,2,1,0:T(8,128)S(1)}, f32[1,1,1,32,128]{4,3,2,1,0:T(8,128)S(1)}, u32[]{:S(2)}, u32[]{:S(2)}) collective-permute-start(f32[1,1,1,32,128]{4,3,2,1,0:T(8,128)S(1)} %slice.282), channel_id=1, source_target_pairs={{0,8},{8,16},{16,24},{1,9},{9,17},{17,25},{2,10},{10,18},{18,26},{... | collective-permute-start | bytes 49160 | tf_op jit(solution)/shard_map/ppermute | solution.py:16
  7.2 59.0 %collective-permute-start.9 = (f32[1,1,1,32,128]{4,3,2,1,0:T(8,128)S(1)}, f32[1,1,1,32,128]{4,3,2,1,0:T(8,128)S(1)}, u32[]{:S(2)}, u32[]{:S(2)}) collective-permute-start(f32[1,1,1,32,128]{4,3,2,1,0:T(8,128)S(1)} %convolution_bitcast_fusion.34), channel_id=1, source_target_pairs={{4,0},{5,1},{6,2},{7,3},{12,8},{13,9},{14,10},{15,11},{20,16},{21,... | collective-permute-start | bytes 49160 | tf_op jit(solution)/shard_map/ppermute | solution.py:17
  8.6 45.2 %collective-permute-start.7 = (f32[1,1,1,32,128]{4,3,2,1,0:T(8,128)S(1)}, f32[1,1,1,32,128]{4,3,2,1,0:T(8,128)S(1)}, u32[]{:S(2)}, u32[]{:S(2)}) collective-permute-start(f32[1,1,1,32,128]{4,3,2,1,0:T(8,128)S(1)} %convolution_bitcast_fusion.35), channel_id=1, source_target_pairs={{8,0},{16,8},{24,16},{9,1},{17,9},{25,17},{10,2},{18,10},{26,18},{... | collective-permute-start | bytes 49160 | tf_op jit(solution)/shard_map/ppermute | solution.py:17
  10.1 65.0 %collective-permute-start.11 = (f32[1,1,1,32,128]{4,3,2,1,0:T(8,128)S(1)}, f32[1,1,1,32,128]{4,3,2,1,0:T(8,128)S(1)}, u32[]{:S(2)}, u32[]{:S(2)}) collective-permute-start(f32[1,1,1,32,128]{4,3,2,1,0:T(8,128)S(1)} %convolution_bitcast_fusion.33), channel_id=1, source_target_pairs={{1,0},{2,1},{3,2},{5,4},{6,5},{7,6},{9,8},{10,9},{11,10},{13,12},{... | collective-permute-start | bytes 49160 | tf_op jit(solution)/shard_map/ppermute | solution.py:17
  13.1 42.0 %copy-start.1 = (f32[1,1,1,32,384]{4,3,2,1,0:T(8,128)S(1)}, f32[1,1,1,32,384]{4,3,2,1,0:T(8,128)}, u32[]{:S(2)}) copy-start(f32[1,1,1,32,384]{4,3,2,1,0:T(8,128)} %param.10) | copy-start | bytes 147460
  17.3 6.0 %collective-permute-start = (f32[1,1,1,32,128]{4,3,2,1,0:T(8,128)S(1)}, f32[1,1,1,32,128]{4,3,2,1,0:T(8,128)S(1)}, u32[]{:S(2)}, u32[]{:S(2)}) collective-permute-start(f32[1,1,1,32,128]{4,3,2,1,0:T(8,128)S(1)} %get-tuple-element.96), channel_id=1, source_target_pairs={{0,8},{8,16},{16,24},{1,9},{9,17},{17,25},{2,10},{10,18},{18,26},{... | collective-permute-start | bytes 49160 | tf_op jit(solution)/shard_map/ppermute | solution.py:16
  23.3 6.0 %collective-permute-start.1 = (f32[1,1,1,32,128]{4,3,2,1,0:T(8,128)S(1)}, f32[1,1,1,32,128]{4,3,2,1,0:T(8,128)S(1)}, u32[]{:S(2)}, u32[]{:S(2)}) collective-permute-start(f32[1,1,1,32,128]{4,3,2,1,0:T(8,128)S(1)} %convolution_bitcast_fusion.40), channel_id=1, source_target_pairs={{8,0},{16,8},{24,16},{9,1},{17,9},{25,17},{10,2},{18,10},{26,18},{... | collective-permute-start | bytes 49160 | tf_op jit(solution)/shard_map/ppermute | solution.py:17
  29.3 2.1 collective-permute-start.2
  31.4 3.1 %collective-permute-start.3 = (f32[1,1,1,32,128]{4,3,2,1,0:T(8,128)S(1)}, f32[1,1,1,32,128]{4,3,2,1,0:T(8,128)S(1)}, u32[]{:S(2)}, u32[]{:S(2)}) collective-permute-start(f32[1,1,1,32,128]{4,3,2,1,0:T(8,128)S(1)} %convolution_bitcast_fusion.38), channel_id=1, source_target_pairs={{4,0},{5,1},{6,2},{7,3},{12,8},{13,9},{14,10},{15,11},{20,16},{21,... | collective-permute-start | bytes 49160 | tf_op jit(solution)/shard_map/ppermute | solution.py:17
  34.5 6.0 %collective-permute-start.4 = (f32[1,1,1,32,128]{4,3,2,1,0:T(8,128)S(1)}, f32[1,1,1,32,128]{4,3,2,1,0:T(8,128)S(1)}, u32[]{:S(2)}, u32[]{:S(2)}) collective-permute-start(f32[1,1,1,32,128]{4,3,2,1,0:T(8,128)S(1)} %get-tuple-element.94), channel_id=1, source_target_pairs={{0,1},{1,2},{2,3},{4,5},{5,6},{6,7},{8,9},{9,10},{10,11},{12,13},{... | collective-permute-start | bytes 49160 | tf_op jit(solution)/shard_map/ppermute | solution.py:16
  40.4 5.9 %collective-permute-start.5 = (f32[1,1,1,32,128]{4,3,2,1,0:T(8,128)S(1)}, f32[1,1,1,32,128]{4,3,2,1,0:T(8,128)S(1)}, u32[]{:S(2)}, u32[]{:S(2)}) collective-permute-start(f32[1,1,1,32,128]{4,3,2,1,0:T(8,128)S(1)} %convolution_bitcast_fusion.36), channel_id=1, source_target_pairs={{1,0},{2,1},{3,2},{5,4},{6,5},{7,6},{9,8},{10,9},{11,10},{13,12},{... | collective-permute-start | bytes 49160 | tf_op jit(solution)/shard_map/ppermute | solution.py:17
  47.0 8.1 %collective-permute-start.12 = (f32[1,1,1,32,128]{4,3,2,1,0:T(8,128)S(1)}, f32[1,1,1,32,128]{4,3,2,1,0:T(8,128)S(1)}, u32[]{:S(2)}, u32[]{:S(2)}) collective-permute-start(f32[1,1,1,32,128]{4,3,2,1,0:T(8,128)S(1)} %slice.346), channel_id=1, source_target_pairs={{0,8},{8,16},{16,24},{1,9},{9,17},{17,25},{2,10},{10,18},{18,26},{... | collective-permute-start | bytes 49160 | tf_op jit(solution)/shard_map/ppermute | solution.py:16
  52.2 24.3 %collective-permute-start.17 = (f32[1,1,1,32,128]{4,3,2,1,0:T(8,128)S(1)}, f32[1,1,1,32,128]{4,3,2,1,0:T(8,128)S(1)}, u32[]{:S(2)}, u32[]{:S(2)}) collective-permute-start(f32[1,1,1,32,128]{4,3,2,1,0:T(8,128)S(1)} %convolution_bitcast_fusion.27), channel_id=1, source_target_pairs={{1,0},{2,1},{3,2},{5,4},{6,5},{7,6},{9,8},{10,9},{11,10},{13,12},{... | collective-permute-start | bytes 49160 | tf_op jit(solution)/shard_map/ppermute | solution.py:17
  53.8 17.2 %collective-permute-start.15 = (f32[1,1,1,32,128]{4,3,2,1,0:T(8,128)S(1)}, f32[1,1,1,32,128]{4,3,2,1,0:T(8,128)S(1)}, u32[]{:S(2)}, u32[]{:S(2)}) collective-permute-start(f32[1,1,1,32,128]{4,3,2,1,0:T(8,128)S(1)} %convolution_bitcast_fusion.29), channel_id=1, source_target_pairs={{4,0},{5,1},{6,2},{7,3},{12,8},{13,9},{14,10},{15,11},{20,16},{21,... | collective-permute-start | bytes 49160 | tf_op jit(solution)/shard_map/ppermute | solution.py:17
  55.2 5.6 %collective-permute-start.13 = (f32[1,1,1,32,128]{4,3,2,1,0:T(8,128)S(1)}, f32[1,1,1,32,128]{4,3,2,1,0:T(8,128)S(1)}, u32[]{:S(2)}, u32[]{:S(2)}) collective-permute-start(f32[1,1,1,32,128]{4,3,2,1,0:T(8,128)S(1)} %convolution_bitcast_fusion.31), channel_id=1, source_target_pairs={{8,0},{16,8},{24,16},{9,1},{17,9},{25,17},{10,2},{18,10},{26,18},{... | collective-permute-start | bytes 49160 | tf_op jit(solution)/shard_map/ppermute | solution.py:17
  60.8 3.0 %collective-permute-start.8 = (f32[1,1,1,32,128]{4,3,2,1,0:T(8,128)S(1)}, f32[1,1,1,32,128]{4,3,2,1,0:T(8,128)S(1)}, u32[]{:S(2)}, u32[]{:S(2)}) collective-permute-start(f32[1,1,1,32,128]{4,3,2,1,0:T(8,128)S(1)} %get-tuple-element.100), channel_id=1, source_target_pairs={{0,4},{1,5},{2,6},{3,7},{8,12},{9,13},{10,14},{11,15},{16,20},{17,... | collective-permute-start | bytes 49160 | tf_op jit(solution)/shard_map/ppermute | solution.py:16
  63.8 7.0 %collective-permute-start.14 = (f32[1,1,1,32,128]{4,3,2,1,0:T(8,128)S(1)}, f32[1,1,1,32,128]{4,3,2,1,0:T(8,128)S(1)}, u32[]{:S(2)}, u32[]{:S(2)}) collective-permute-start(f32[1,1,1,32,128]{4,3,2,1,0:T(8,128)S(1)} %get-tuple-element.90), channel_id=1, source_target_pairs={{0,4},{1,5},{2,6},{3,7},{8,12},{9,13},{10,14},{11,15},{16,20},{17,... | collective-permute-start | bytes 49160 | tf_op jit(solution)/shard_map/ppermute | solution.py:16
  66.2 8.7 %collective-permute-start.10 = (f32[1,1,1,32,128]{4,3,2,1,0:T(8,128)S(1)}, f32[1,1,1,32,128]{4,3,2,1,0:T(8,128)S(1)}, u32[]{:S(2)}, u32[]{:S(2)}) collective-permute-start(f32[1,1,1,32,128]{4,3,2,1,0:T(8,128)S(1)} %get-tuple-element.98), channel_id=1, source_target_pairs={{0,1},{1,2},{2,3},{4,5},{5,6},{6,7},{8,9},{9,10},{10,11},{12,13},{... | collective-permute-start | bytes 49160 | tf_op jit(solution)/shard_map/ppermute | solution.py:16
  71.0 5.4 %collective-permute-start.16 = (f32[1,1,1,32,128]{4,3,2,1,0:T(8,128)S(1)}, f32[1,1,1,32,128]{4,3,2,1,0:T(8,128)S(1)}, u32[]{:S(2)}, u32[]{:S(2)}) collective-permute-start(f32[1,1,1,32,128]{4,3,2,1,0:T(8,128)S(1)} %get-tuple-element.88), channel_id=1, source_target_pairs={{0,1},{1,2},{2,3},{4,5},{5,6},{6,7},{8,9},{9,10},{10,11},{12,13},{... | collective-permute-start | bytes 49160 | tf_op jit(solution)/shard_map/ppermute | solution.py:16
  77.7 8.7 %collective-permute-start.18 = (f32[1,1,1,32,128]{4,3,2,1,0:T(8,128)S(1)}, f32[1,1,1,32,128]{4,3,2,1,0:T(8,128)S(1)}, u32[]{:S(2)}, u32[]{:S(2)}) collective-permute-start(f32[1,1,1,32,128]{4,3,2,1,0:T(8,128)S(1)} %slice.352), channel_id=1, source_target_pairs={{0,8},{8,16},{16,24},{1,9},{9,17},{17,25},{2,10},{10,18},{18,26},{... | collective-permute-start | bytes 49160 | tf_op jit(solution)/shard_map/ppermute | solution.py:16
  82.5 16.0 %collective-permute-start.23 = (f32[1,1,1,32,128]{4,3,2,1,0:T(8,128)S(1)}, f32[1,1,1,32,128]{4,3,2,1,0:T(8,128)S(1)}, u32[]{:S(2)}, u32[]{:S(2)}) collective-permute-start(f32[1,1,1,32,128]{4,3,2,1,0:T(8,128)S(1)} %convolution_bitcast_fusion.21), channel_id=1, source_target_pairs={{1,0},{2,1},{3,2},{5,4},{6,5},{7,6},{9,8},{10,9},{11,10},{13,12},{... | collective-permute-start | bytes 49160 | tf_op jit(solution)/shard_map/ppermute | solution.py:17
  83.8 14.5 %collective-permute-start.21 = (f32[1,1,1,32,128]{4,3,2,1,0:T(8,128)S(1)}, f32[1,1,1,32,128]{4,3,2,1,0:T(8,128)S(1)}, u32[]{:S(2)}, u32[]{:S(2)}) collective-permute-start(f32[1,1,1,32,128]{4,3,2,1,0:T(8,128)S(1)} %convolution_bitcast_fusion.23), channel_id=1, source_target_pairs={{4,0},{5,1},{6,2},{7,3},{12,8},{13,9},{14,10},{15,11},{20,16},{21,... | collective-permute-start | bytes 49160 | tf_op jit(solution)/shard_map/ppermute | solution.py:17
  85.1 5.7 %collective-permute-start.19 = (f32[1,1,1,32,128]{4,3,2,1,0:T(8,128)S(1)}, f32[1,1,1,32,128]{4,3,2,1,0:T(8,128)S(1)}, u32[]{:S(2)}, u32[]{:S(2)}) collective-permute-start(f32[1,1,1,32,128]{4,3,2,1,0:T(8,128)S(1)} %convolution_bitcast_fusion.25), channel_id=1, source_target_pairs={{8,0},{16,8},{24,16},{9,1},{17,9},{25,17},{10,2},{18,10},{26,18},{... | collective-permute-start | bytes 49160 | tf_op jit(solution)/shard_map/ppermute | solution.py:17
  90.7 7.6 %collective-permute-start.22 = (f32[1,1,1,32,128]{4,3,2,1,0:T(8,128)S(1)}, f32[1,1,1,32,128]{4,3,2,1,0:T(8,128)S(1)}, u32[]{:S(2)}, u32[]{:S(2)}) collective-permute-start(f32[1,1,1,32,128]{4,3,2,1,0:T(8,128)S(1)} %get-tuple-element.91), channel_id=1, source_target_pairs={{0,1},{1,2},{2,3},{4,5},{5,6},{6,7},{8,9},{9,10},{10,11},{12,13},{... | collective-permute-start | bytes 49160 | tf_op jit(solution)/shard_map/ppermute | solution.py:16
  95.5 2.6 collective-permute-start.20
  99.4 6.8 %collective-permute-start.24 = (f32[1,1,1,32,128]{4,3,2,1,0:T(8,128)S(1)}, f32[1,1,1,32,128]{4,3,2,1,0:T(8,128)S(1)}, u32[]{:S(2)}, u32[]{:S(2)}) collective-permute-start(f32[1,1,1,32,128]{4,3,2,1,0:T(8,128)S(1)} %slice.361), channel_id=1, source_target_pairs={{0,8},{8,16},{16,24},{1,9},{9,17},{17,25},{2,10},{10,18},{18,26},{... | collective-permute-start | bytes 49160 | tf_op jit(solution)/shard_map/ppermute | solution.py:16
  102.3 15.7 %collective-permute-start.29 = (f32[1,1,1,32,128]{4,3,2,1,0:T(8,128)S(1)}, f32[1,1,1,32,128]{4,3,2,1,0:T(8,128)S(1)}, u32[]{:S(2)}, u32[]{:S(2)}) collective-permute-start(f32[1,1,1,32,128]{4,3,2,1,0:T(8,128)S(1)} %convolution_bitcast_fusion.15), channel_id=1, source_target_pairs={{1,0},{2,1},{3,2},{5,4},{6,5},{7,6},{9,8},{10,9},{11,10},{13,12},{... | collective-permute-start | bytes 49160 | tf_op jit(solution)/shard_map/ppermute | solution.py:17
  103.6 14.2 %collective-permute-start.27 = (f32[1,1,1,32,128]{4,3,2,1,0:T(8,128)S(1)}, f32[1,1,1,32,128]{4,3,2,1,0:T(8,128)S(1)}, u32[]{:S(2)}, u32[]{:S(2)}) collective-permute-start(f32[1,1,1,32,128]{4,3,2,1,0:T(8,128)S(1)} %convolution_bitcast_fusion.17), channel_id=1, source_target_pairs={{4,0},{5,1},{6,2},{7,3},{12,8},{13,9},{14,10},{15,11},{20,16},{21,... | collective-permute-start | bytes 49160 | tf_op jit(solution)/shard_map/ppermute | solution.py:17
  104.9 5.7 %collective-permute-start.25 = (f32[1,1,1,32,128]{4,3,2,1,0:T(8,128)S(1)}, f32[1,1,1,32,128]{4,3,2,1,0:T(8,128)S(1)}, u32[]{:S(2)}, u32[]{:S(2)}) collective-permute-start(f32[1,1,1,32,128]{4,3,2,1,0:T(8,128)S(1)} %convolution_bitcast_fusion.19), channel_id=1, source_target_pairs={{8,0},{16,8},{24,16},{9,1},{17,9},{25,17},{10,2},{18,10},{26,18},{... | collective-permute-start | bytes 49160 | tf_op jit(solution)/shard_map/ppermute | solution.py:17
  110.5 7.3 %collective-permute-start.28 = (f32[1,1,1,32,128]{4,3,2,1,0:T(8,128)S(1)}, f32[1,1,1,32,128]{4,3,2,1,0:T(8,128)S(1)}, u32[]{:S(2)}, u32[]{:S(2)}) collective-permute-start(f32[1,1,1,32,128]{4,3,2,1,0:T(8,128)S(1)} %get-tuple-element.78), channel_id=1, source_target_pairs={{0,1},{1,2},{2,3},{4,5},{5,6},{6,7},{8,9},{9,10},{10,11},{12,13},{... | collective-permute-start | bytes 49160 | tf_op jit(solution)/shard_map/ppermute | solution.py:16
  115.1 2.6 collective-permute-start.26
  171.5 15.3 %collective-permute-start.30 = (f32[1,1,1,32,128]{4,3,2,1,0:T(8,128)S(1)}, f32[1,1,1,32,128]{4,3,2,1,0:T(8,128)S(1)}, u32[]{:S(2)}, u32[]{:S(2)}) collective-permute-start(f32[1,1,1,32,128]{4,3,2,1,0:T(8,128)S(1)} %get-tuple-element.71), channel_id=1, source_target_pairs={{0,8},{8,16},{16,24},{1,9},{9,17},{17,25},{2,10},{10,18},{18,26},{... | collective-permute-start | bytes 49160 | tf_op jit(solution)/shard_map/while/body/eval_jaxpr/ppermute | solution.py:16
  178.3 12.4 %collective-permute-start.35 = (f32[1,1,1,32,128]{4,3,2,1,0:T(8,128)S(1)}, f32[1,1,1,32,128]{4,3,2,1,0:T(8,128)S(1)}, u32[]{:S(2)}, u32[]{:S(2)}) collective-permute-start(f32[1,1,1,32,128]{4,3,2,1,0:T(8,128)S(1)} %convolution_bitcast_fusion.9), channel_id=1, source_target_pairs={{1,0},{2,1},{3,2},{5,4},{6,5},{7,6},{9,8},{10,9},{11,10},{13,12},{... | collective-permute-start | bytes 49160 | tf_op jit(solution)/shard_map/while/body/eval_jaxpr/ppermute | solution.py:17
  179.6 10.9 %collective-permute-start.33 = (f32[1,1,1,32,128]{4,3,2,1,0:T(8,128)S(1)}, f32[1,1,1,32,128]{4,3,2,1,0:T(8,128)S(1)}, u32[]{:S(2)}, u32[]{:S(2)}) collective-permute-start(f32[1,1,1,32,128]{4,3,2,1,0:T(8,128)S(1)} %convolution_bitcast_fusion.11), channel_id=1, source_target_pairs={{4,0},{5,1},{6,2},{7,3},{12,8},{13,9},{14,10},{15,11},{20,16},{21,... | collective-permute-start | bytes 49160 | tf_op jit(solution)/shard_map/while/body/eval_jaxpr/ppermute | solution.py:17
  180.9 8.8 %collective-permute-start.31 = (f32[1,1,1,32,128]{4,3,2,1,0:T(8,128)S(1)}, f32[1,1,1,32,128]{4,3,2,1,0:T(8,128)S(1)}, u32[]{:S(2)}, u32[]{:S(2)}) collective-permute-start(f32[1,1,1,32,128]{4,3,2,1,0:T(8,128)S(1)} %convolution_bitcast_fusion.13), channel_id=1, source_target_pairs={{8,0},{16,8},{24,16},{9,1},{17,9},{25,17},{10,2},{18,10},{26,18},{... | collective-permute-start | bytes 49160 | tf_op jit(solution)/shard_map/while/body/eval_jaxpr/ppermute | solution.py:17
  182.2 8.3 %collective-permute-start.34 = (f32[1,1,1,32,128]{4,3,2,1,0:T(8,128)S(1)}, f32[1,1,1,32,128]{4,3,2,1,0:T(8,128)S(1)}, u32[]{:S(2)}, u32[]{:S(2)}) collective-permute-start(f32[1,1,1,32,128]{4,3,2,1,0:T(8,128)S(1)} %get-tuple-element.69), channel_id=1, source_target_pairs={{0,1},{1,2},{2,3},{4,5},{5,6},{6,7},{8,9},{9,10},{10,11},{12,13},{... | collective-permute-start | bytes 49160 | tf_op jit(solution)/shard_map/while/body/eval_jaxpr/ppermute | solution.py:16
  186.8 3.6 %collective-permute-start.32 = (f32[1,1,1,32,128]{4,3,2,1,0:T(8,128)S(1)}, f32[1,1,1,32,128]{4,3,2,1,0:T(8,128)S(1)}, u32[]{:S(2)}, u32[]{:S(2)}) collective-permute-start(f32[1,1,1,32,128]{4,3,2,1,0:T(8,128)S(1)} %get-tuple-element.70), channel_id=1, source_target_pairs={{0,4},{1,5},{2,6},{3,7},{8,12},{9,13},{10,14},{11,15},{16,20},{17,... | collective-permute-start | bytes 49160 | tf_op jit(solution)/shard_map/while/body/eval_jaxpr/ppermute | solution.py:16
  191.7 8.6 %collective-permute-start.36 = (f32[1,1,1,32,128]{4,3,2,1,0:T(8,128)S(1)}, f32[1,1,1,32,128]{4,3,2,1,0:T(8,128)S(1)}, u32[]{:S(2)}, u32[]{:S(2)}) collective-permute-start(f32[1,1,1,32,128]{4,3,2,1,0:T(8,128)S(1)} %slice.382), channel_id=1, source_target_pairs={{0,8},{8,16},{16,24},{1,9},{9,17},{17,25},{2,10},{10,18},{18,26},{... | collective-permute-start | bytes 49160 | tf_op jit(solution)/shard_map/while/body/eval_jaxpr/ppermute | solution.py:16
  195.9 16.2 %collective-permute-start.41 = (f32[1,1,1,32,128]{4,3,2,1,0:T(8,128)S(1)}, f32[1,1,1,32,128]{4,3,2,1,0:T(8,128)S(1)}, u32[]{:S(2)}, u32[]{:S(2)}) collective-permute-start(f32[1,1,1,32,128]{4,3,2,1,0:T(8,128)S(1)} %convolution_bitcast_fusion.3), channel_id=1, source_target_pairs={{1,0},{2,1},{3,2},{5,4},{6,5},{7,6},{9,8},{10,9},{11,10},{13,12},{... | collective-permute-start | bytes 49160 | tf_op jit(solution)/shard_map/while/body/eval_jaxpr/ppermute | solution.py:17
  197.2 14.7 %collective-permute-start.39 = (f32[1,1,1,32,128]{4,3,2,1,0:T(8,128)S(1)}, f32[1,1,1,32,128]{4,3,2,1,0:T(8,128)S(1)}, u32[]{:S(2)}, u32[]{:S(2)}) collective-permute-start(f32[1,1,1,32,128]{4,3,2,1,0:T(8,128)S(1)} %convolution_bitcast_fusion.5), channel_id=1, source_target_pairs={{4,0},{5,1},{6,2},{7,3},{12,8},{13,9},{14,10},{15,11},{20,16},{21,... | collective-permute-start | bytes 49160 | tf_op jit(solution)/shard_map/while/body/eval_jaxpr/ppermute | solution.py:17
  198.5 6.0 %collective-permute-start.37 = (f32[1,1,1,32,128]{4,3,2,1,0:T(8,128)S(1)}, f32[1,1,1,32,128]{4,3,2,1,0:T(8,128)S(1)}, u32[]{:S(2)}, u32[]{:S(2)}) collective-permute-start(f32[1,1,1,32,128]{4,3,2,1,0:T(8,128)S(1)} %convolution_bitcast_fusion.7), channel_id=1, source_target_pairs={{8,0},{16,8},{24,16},{9,1},{17,9},{25,17},{10,2},{18,10},{26,18},{... | collective-permute-start | bytes 49160 | tf_op jit(solution)/shard_map/while/body/eval_jaxpr/ppermute | solution.py:17
  204.6 7.4 %collective-permute-start.40 = (f32[1,1,1,32,128]{4,3,2,1,0:T(8,128)S(1)}, f32[1,1,1,32,128]{4,3,2,1,0:T(8,128)S(1)}, u32[]{:S(2)}, u32[]{:S(2)}) collective-permute-start(f32[1,1,1,32,128]{4,3,2,1,0:T(8,128)S(1)} %get-tuple-element.63), channel_id=1, source_target_pairs={{0,1},{1,2},{2,3},{4,5},{5,6},{6,7},{8,9},{9,10},{10,11},{12,13},{... | collective-permute-start | bytes 49160 | tf_op jit(solution)/shard_map/while/body/eval_jaxpr/ppermute | solution.py:16
  209.1 2.7 %collective-permute-start.38 = (f32[1,1,1,32,128]{4,3,2,1,0:T(8,128)S(1)}, f32[1,1,1,32,128]{4,3,2,1,0:T(8,128)S(1)}, u32[]{:S(2)}, u32[]{:S(2)}) collective-permute-start(f32[1,1,1,32,128]{4,3,2,1,0:T(8,128)S(1)} %get-tuple-element.65), channel_id=1, source_target_pairs={{0,4},{1,5},{2,6},{3,7},{8,12},{9,13},{10,14},{11,15},{16,20},{17,... | collective-permute-start | bytes 49160 | tf_op jit(solution)/shard_map/while/body/eval_jaxpr/ppermute | solution.py:16
where the time goes:
time: 266 us; the launch traced here: 264 us
  starting transfers between devices  103 us (39%)
  blocking collectives  80.8 us (30%)
  waiting for transfers between devices  35.9 us (13%)
  other arithmetic  25.6 us (10%)
  matrix products  14.1 us (5%)
  between operations  2.66 us (1%)
    ppermute x21, starting transfers between devices, extended(): before = lax.ppermute(last, axis, up)  75.7 us
    psum x1, blocking collectives, iterate(): lax.psum((pairing(projected, residual, face_width), pairing(projected, pr...  40.7 us
    psum x1, blocking collectives, local(): lax.psum((pairing(projected, residual, face_width), pairing(projected, pr...  40.1 us
    ppermute x21, waiting for transfers between devices, extended(): after = lax.ppermute(leading, axis, down)  27.7 us
    ppermute x21, starting transfers between devices, extended(): after = lax.ppermute(leading, axis, down)  27.3 us
    another operation x9, other arithmetic, cholesky_solve(): factor = jnp.linalg.cholesky(matrix)  10.8 us
    another operation x6, other arithmetic, cholesky_solve(): return jax.scipy.linalg.cho_solve((factor, True), right_side)  9.32 us
    ppermute x21, waiting for transfers between devices, extended(): before = lax.ppermute(last, axis, up)  8.2 us
  transfers between devices with their start and end apart: 42, of which 16 were waited for; matrix products, arithmetic and copies ran while one was open for 5% of the time, Pallas kernels for 0%

commit v1 on v0

v1 whole, which is shorter than its diff:
```python
import functools

import jax
import jax.numpy as jnp
from jax import lax
from jax.experimental import pallas as pl
from jax.experimental.pallas import tpu as pltpu
from jax.sharding import PartitionSpec as P

MESH = pl.DeviceIdType.MESH
HIGH = lax.Precision.HIGHEST
NN = (((1,), (0,)), ((), ()))
NT = (((1,), (1,)), ((), ()))
TN = (((0,), (0,)), ((), ()))


def mul(a, b, dims=NN):
    return lax.dot_general(a, b, dims, precision=HIGH, preferred_element_type=jnp.float32)


def eliminate(system, size):
    rows = lax.broadcasted_iota(jnp.int32, system.shape, 0)
    for k in range(size):
        row = system[k : k + 1, :]
        column = system[:, k : k + 1]
        scaled = row / row[:, k : k + 1]
        system = jnp.where(rows == k, scaled, system - column * scaled)
    return system[:, size:]


def identity(size):
    return (
        lax.broadcasted_iota(jnp.int32, (size, size), 0)
        == lax.broadcasted_iota(jnp.int32, (size, size), 1)
    ).astype(jnp.float32)


def packed(gram, width):
    groups = max(1, width // gram.shape[1])
    depth = gram.shape[0] // groups
    return jnp.concatenate([gram[g * depth : (g + 1) * depth] for g in range(groups)], axis=1)


def unpacked(tile, size):
    groups = max(1, tile.shape[1] // size)
    return jnp.concatenate([tile[:, g * size : (g + 1) * size] for g in range(groups)], axis=0)


def kernel(
    extents,
    operator_hbm,
    load_ref,
    modes_ref,
    coarse_ref,
    count_ref,
    maps_ref,
    multipliers_ref,
    residual_ref,
    raw,
    ordered,
    own_modes,
    minus_modes,
    all_modes,
    padded_load,
    coefficients,
    face_out,
    face_in,
    load_in,
    plane_sums,
    line_sums,
    raw_sem,
    coefficient_send,
    coefficient_recv,
    face_send,
    face_recv,
    mode_send,
    mode_recv,
    load_send,
    load_recv,
    plane_send,
    plane_recv,
    line_send,
    line_recv,
):
    nx, ny, nz = extents
    cases = load_ref.shape[0]
    width = load_ref.shape[1] // 3
    modes = modes_ref.shape[0]
    padded = own_modes.shape[0]
    here = (lax.axis_index("gx"), lax.axis_index("gy"), lax.axis_index("gz"))
    ix, iy, iz = here
    plane = nx * ny
    slot = ix * ny + iy

    fetch = pltpu.make_async_copy(operator_hbm, raw, raw_sem)
    fetch.start()

    for phase in range(3):
        coefficients[phase] = jnp.zeros(coefficients.shape[1:], jnp.float32)
    all_modes[...] = jnp.zeros(all_modes.shape, jnp.float32)
    own_modes[...] = jnp.zeros(own_modes.shape, jnp.float32)
    padded_load[...] = jnp.zeros(padded_load.shape, jnp.float32)

    def plane_peer(offset):
        other = lax.rem(slot + offset, plane)
        return (lax.div(other, ny), lax.rem(other, ny), iz)

    def line_peer(offset):
        return (ix, iy, lax.rem(iz + offset, nz))

    barrier = pltpu.get_barrier_semaphore()
    for offset in range(1, plane):
        pl.semaphore_signal(barrier, inc=1, device_id=plane_peer(offset), device_id_type=MESH)
    for offset in range(1, nz):
        pl.semaphore_signal(barrier, inc=1, device_id=line_peer(offset), device_id_type=MESH)

    exists = []
    neighbour = []
    for d in range(3):
        exists.append(here[d] > 0)
        exists.append(here[d] < extents[d] - 1)
        for step in (-1, 1):
            neighbour.append(tuple(here[a] + (step if a == d else 0) for a in range(3)))
    flags = [jnp.where(e, 1, 0).astype(jnp.int32) for e in exists]

    def face(values, f):
        return values[:, f * width : (f + 1) * width]

    def masked(values, f):
        return jnp.where(jnp.full(values.shape, flags[f], jnp.int32) == 1, values, 0.0)

    waits = []

    def remote(source, target, send, recv, where):
        return pltpu.make_async_remote_copy(
            src_ref=source,
            dst_ref=target,
            send_sem=send,
            recv_sem=recv,
            device_id=where,
            device_id_type=MESH,
        )

    def start_to(f, copy):
        pl.when(exists[f])(copy.start)
        waits.append((f, copy))

    count = count_ref[0, 0]
    lines = lax.broadcasted_iota(jnp.int32, (width, width), 0)
    orders = [(lines == maps_ref[d : d + 1, :]).astype(jnp.float32) for d in range(3)]
    own_modes[0:modes, :] = modes_ref[...]
    padded_load[0:modes, 0:cases] = coarse_ref[...]
    raw_modes = jnp.where(
        lax.broadcasted_iota(jnp.int32, own_modes.shape, 0) < count, own_modes[...], 0.0
    )
    pieces = []
    for d in range(3):
        pieces.append(masked(mul(face(raw_modes, 2 * d), orders[d], NT), 2 * d))
        pieces.append(masked(face(raw_modes, 2 * d + 1), 2 * d + 1))
    mode_rows = jnp.concatenate(pieces, axis=1)
    own_modes[...] = mode_rows
    minus_modes[...] = -mode_rows
    all_modes[0:padded, :] = mode_rows
    inactive = lax.broadcasted_iota(jnp.int32, (padded, padded), 0) >= count
    normal = mul(mode_rows, mode_rows, NT) + jnp.where(inactive, identity(padded), 0.0)
    coarse_inverse = eliminate(jnp.concatenate([normal, identity(padded)], axis=1), padded)
    active_load = jnp.where(
        lax.broadcasted_iota(jnp.int32, padded_load.shape, 0) < count, padded_load[...], 0.0
    )
    coefficients[0, 0:padded, :] = mul(coarse_inverse, active_load)

    pl.semaphore_wait(barrier, plane - 1 + nz - 1)

    def slot_of(phase, f):
        return coefficients.at[phase, pl.ds((1 + f) * padded, padded), :]

    def columns(ref, f):
        return ref.at[:, pl.ds(f * width, width)]

    def send_coefficients(phase):
        for f in range(6):
            start_to(
                f,
                remote(
                    coefficients.at[phase, pl.ds(0, padded), :],
                    slot_of(phase, f ^ 1),
                    coefficient_send.at[phase, f],
                    coefficient_recv.at[phase, f ^ 1],
                    neighbour[f],
                ),
            )

    def wait_coefficients(phase):
        for f in range(6):
            copy = remote(
                coefficients.at[phase, pl.ds(0, padded), :],
                slot_of(phase, f),
                coefficient_send.at[phase, f],
                coefficient_recv.at[phase, f],
                neighbour[f],
            )
            pl.when(exists[f])(copy.wait_recv)

    def coarse_field(phase):
        return mul(coefficients[phase][:, 0:cases], all_modes[...], TN)

    def send_faces(phase):
        for f in range(6):
            start_to(
                f,
                remote(
                    face_out.at[phase, f],
                    face_in.at[phase, f ^ 1],
                    face_send.at[phase, f],
                    face_recv.at[phase, f ^ 1],
                    neighbour[f],
                ),
            )

    def wait_faces(phase):
        for f in range(6):
            copy = remote(
                face_out.at[phase, f],
                face_in.at[phase, f],
                face_send.at[phase, f],
                face_recv.at[phase, f],
                neighbour[f],
            )
            pl.when(exists[f])(copy.wait_recv)

    def assembled(phase):
        return jnp.concatenate(
            [masked(face_out[phase, f] - face_in[phase, f], f) for f in range(6)], axis=1
        )

    def apply_local(values):
        head = values.astype(jnp.bfloat16)
        tail = (values - head.astype(jnp.float32)).astype(jnp.bfloat16)
        both = jnp.dot(
            jnp.concatenate([head, tail], axis=0),
            ordered[...],
            preferred_element_type=jnp.float32,
        )
        return both[0:cases] + both[cases:]

    def keep_faces(phase, values):
        for f in range(6):
            face_out[phase, f] = face(values, f)

    def owned(values):
        return jnp.concatenate([face(values, 1), face(values, 3), face(values, 5)], axis=1)

    for f in range(6):
        start_to(
            f,
            remote(
                columns(minus_modes, f),
                all_modes.at[pl.ds((1 + (f ^ 1)) * padded, padded), pl.ds((f ^ 1) * width, width)],
                mode_send.at[f],
                mode_recv.at[f ^ 1],
                neighbour[f],
            ),
        )
    send_coefficients(0)
    for d in range(3):
        start_to(
            2 * d + 1,
            remote(
                columns(load_ref, d),
                load_in.at[d],
                load_send.at[d],
                load_recv.at[d],
                neighbour[2 * d + 1],
            ),
        )

    fetch.wait()
    narrow = [order.astype(jnp.bfloat16) for order in orders]
    for d in range(3):
        low = 2 * d * width
        raw[pl.ds(low, width), :] = jnp.dot(
            narrow[d], raw[pl.ds(low, width), :], preferred_element_type=jnp.float32
        ).astype(jnp.bfloat16)
    for d in range(3):
        low = 2 * d * width
        ordered[:, low : low + width] = lax.dot_general(
            raw[:, low : low + width], narrow[d], NT, preferred_element_type=jnp.float32
        ).astype(jnp.bfloat16)
        ordered[:, low + width : low + 2 * width] = raw[:, low + width : low + 2 * width]
    inverse_modes = mul(coarse_inverse, mode_rows)

    for f in range(6):
        copy = remote(
            columns(minus_modes, f),
            all_modes.at[pl.ds((1 + f) * padded, padded), pl.ds(f * width, width)],
            mode_send.at[f],
            mode_recv.at[f],
            neighbour[f],
        )
        pl.when(exists[f])(copy.wait_recv)
    wait_coefficients(0)
    initial = coarse_field(0)
    product = apply_local(initial)
    keep_faces(0, product)
    send_faces(0)
    for d in range(3):
        copy = remote(
            columns(load_ref, d),
            load_in.at[d],
            load_send.at[d],
            load_recv.at[d],
            neighbour[2 * d],
        )
        pl.when(exists[2 * d])(copy.wait_recv)
    right = []
    for d in range(3):
        right.append(masked(-load_in[d], 2 * d))
        right.append(masked(load_ref[:, d * width : (d + 1) * width], 2 * d + 1))
    right = jnp.concatenate(right, axis=1)
    wait_faces(0)
    residual = right - assembled(0)

    def precondition(phase, values):
        coefficients[phase, 0:padded, 0:cases] = mul(inverse_modes, values, NT)
        send_coefficients(phase)

    def preconditioned(phase, values):
        wait_coefficients(phase)
        return values - 0.25 * coarse_field(phase)

    def sum_start(which, tile):
        plane_sums[which, slot] = tile
        copies = []
        for offset in range(1, plane):
            copy = remote(
                plane_sums.at[which, slot],
                plane_sums.at[which, slot],
                plane_send.at[which, offset],
                plane_recv.at[which, offset],
                plane_peer(offset),
            )
            copy.start()
            copies.append(copy)
        return copies

    def sum_middle(which, copies):
        for offset in range(1, plane):
            copy = remote(
                plane_sums.at[which, slot],
                plane_sums.at[which, lax.rem(slot + plane - offset, plane)],
                plane_send.at[which, offset],
                plane_recv.at[which, offset],
                plane_peer(offset),
            )
            copy.wait_recv()
        total = plane_sums[which, 0]
        for other in range(1, plane):
            total = total + plane_sums[which, other]
        line_sums[which, iz] = total
        for offset in range(1, nz):
            copy = remote(
                line_sums.at[which, iz],
                line_sums.at[which, iz],
                line_send.at[which, offset],
                line_recv.at[which, offset],
                line_peer(offset),
            )
            copy.start()
            copies.append(copy)

    def sum_end(which):
        for offset in range(1, nz):
            copy = remote(
                line_sums.at[which, iz],
                line_sums.at[which, lax.rem(iz + nz - offset, nz)],
                line_send.at[which, offset],
                line_recv.at[which, offset],
                line_peer(offset),
            )
            copy.wait_recv()
        total = line_sums[which, 0]
        for other in range(1, nz):
            total = total + line_sums[which, other]
        half = total.shape[0] // 2
        return unpacked(total[0:half], cases), unpacked(total[half:], cases)

    precondition(1, residual)
    start = preconditioned(1, residual)
    product = apply_local(start)
    keep_faces(1, product)
    send_faces(1)
    early = sum_start(
        0,
        jnp.concatenate(
            [
                packed(mul(owned(start), owned(residual), NT), width),
                packed(mul(start, product, NT), width),
            ],
            axis=0,
        ),
    )
    wait_faces(1)
    image = assembled(1)
    precondition(2, image)
    sum_middle(0, early)
    second = preconditioned(2, image)
    product = apply_local(second)
    keep_faces(2, product)
    late = sum_start(
        1,
        jnp.concatenate(
            [
                packed(mul(owned(second), owned(image), NT), width),
                packed(mul(second, product, NT), width),
            ],
            axis=0,
        ),
    )
    send_faces(2)
    gram, energy = sum_end(0)
    inverse = eliminate(jnp.concatenate([energy, identity(cases)], axis=1), cases)
    alpha = mul(inverse, gram)
    sum_middle(1, late)
    wait_faces(2)
    second_image = assembled(2)
    cross, last = sum_end(1)
    carried = mul(inverse, cross)
    schur = last - mul(cross, carried)
    right_side = mul(cross, alpha) - energy
    tail = eliminate(jnp.concatenate([schur, right_side], axis=1), cases)
    head = alpha + mul(carried, tail)
    both = jnp.concatenate([head, -tail], axis=0)
    multipliers_ref[...] = owned(initial) + mul(
        both, jnp.concatenate([owned(start), owned(second)], axis=0), TN
    )
    residual_ref[...] = owned(residual) - mul(
        both, jnp.concatenate([owned(image), owned(second_image)], axis=0), TN
    )

    for f, copy in waits:
        pl.when(exists[f])(copy.wait_send)
    for copy in early + late:
        copy.wait_send()


def local(extents, dual_operators, dual_load, rigid_modes, coarse_load, mode_counts, face_maps):
    size = dual_operators.shape[-1]
    cases = dual_load.shape[-2]
    width = dual_load.shape[-1] // 3
    modes = rigid_modes.shape[-2]
    padded = -(-modes // 8) * 8
    nx, ny, nz = extents
    plane = nx * ny
    tile = 2 * cases // max(1, width // cases)
    f32 = jnp.float32
    vmem = pl.BlockSpec(memory_space=pltpu.VMEM)
    dma = pltpu.SemaphoreType.DMA
    out = jax.ShapeDtypeStruct((cases, 3 * width), f32)
    multipliers, residual = pl.pallas_call(
        functools.partial(kernel, extents),
        out_shape=(out, out),
        in_specs=[
            pl.BlockSpec(memory_space=pl.ANY),
            vmem,
            vmem,
            vmem,
            pl.BlockSpec(memory_space=pltpu.SMEM),
            vmem,
        ],
        out_specs=(vmem, vmem),
        scratch_shapes=[
            pltpu.VMEM((size, size), dual_operators.dtype),
            pltpu.VMEM((size, size), dual_operators.dtype),
            pltpu.VMEM((padded, size), f32),
            pltpu.VMEM((padded, size), f32),
            pltpu.VMEM((7 * padded, size), f32),
            pltpu.VMEM((padded, width), f32),
            pltpu.VMEM((3, 7 * padded, width), f32),
            pltpu.VMEM((3, 6, cases, width), f32),
            pltpu.VMEM((3, 6, cases, width), f32),
            pltpu.VMEM((3, cases, width), f32),
            pltpu.VMEM((2, plane, tile, width), f32),
            pltpu.VMEM((2, nz, tile, width), f32),
            dma,
            dma((3, 6)),
            dma((3, 6)),
            dma((3, 6)),
            dma((3, 6)),
            dma((6,)),
            dma((6,)),
            dma((3,)),
            dma((3,)),
            dma((2, plane)),
            dma((2, plane)),
            dma((2, nz)),
            dma((2, nz)),
        ],
        compiler_params=pltpu.CompilerParams(collective_id=0, has_side_effects=True),
    )(
        dual_operators.reshape(size, size),
        dual_load.reshape(cases, 3 * width),
        rigid_modes.reshape(modes, size),
        coarse_load.reshape(modes, cases),
        mode_counts.reshape(1, 1),
        face_maps.reshape(3, width),
    )
    shape = (1, 1, 1, cases, 3 * width)
    return multipliers.reshape(shape), residual.reshape(shape)


def solution(mesh):
    extents = (mesh.shape["gx"], mesh.shape["gy"], mesh.shape["gz"])
    spec = P("gx", "gy", "gz", None, None)
    return jax.shard_map(
        functools.partial(local, extents),
        mesh=mesh,
        in_specs=(spec, spec, spec, spec, P("gx", "gy", "gz"), spec),
        out_specs=(spec, spec),
        check_vma=False,
    )
```

time: 266 us -> 45 us (0.17)
  starting transfers between devices: 103 us -> 0 us
  blocking collectives: 80.8 us -> 0 us
  Pallas kernels: 0 us -> 36.6 us
  waiting for transfers between devices: 35.9 us -> 0 us
  other arithmetic: 25.6 us -> 0 us
  matrix products: 14.1 us -> 0 us
  local copies, waits for them, and re-layouts: 2.41 us -> 6.73 us
    ppermute x42 -> x0, starting transfers between devices: 103 us -> none  [the longest x21 75.7 us: extended(): before = lax.ppermute(last, axis, up)]
    psum x2 -> x0, blocking collectives: 80.8 us -> none  [the longest x1 40.7 us: iterate(): lax.psum((pairing(projected, residual, face_width), pairing(projected, pr...]
    pallas_call x0 -> x1, Pallas kernels: none -> 36.6 us  [local(): pl.pallas_call(functools.partial(kernel, extents), out_shape=(out, out),...]
    ppermute x42 -> x0, waiting for transfers between devices: 35.9 us -> none  [the longest x21 27.7 us: extended(): after = lax.ppermute(leading, axis, down)]
    another operation x20 -> x0, other arithmetic: 22.5 us -> none  [the longest x9 10.8 us: cholesky_solve(): factor = jnp.linalg.cholesky(matrix)]
    dot_general x70 -> x0, matrix products: 12.7 us -> none  [the longest x21 3.37 us: backward_order(): jnp.einsum('xyzrk,xyzjk->xyzrj', values, permuter, precision=lax.Precisio...]
    unnamed x19 -> x5, local copies, waits for them, and re-layouts: 0.15 us -> 6.73 us
  transfers between devices with their start and end apart: 42 -> 0, of which waited for: 16 -> 0; matrix products, arithmetic and copies ran while one was open for 5% -> 0% of each run, Pallas kernels for 0% -> 0%
where the time goes in v1:
time: 45 us; the launch traced here: 44.6 us
  Pallas kernels  36.6 us (81%)
  local copies, waits for them, and re-layouts  6.73 us (15%)
  between operations  1.29 us (3%)
    pallas_call x1, Pallas kernels, local(): pl.pallas_call(functools.partial(kernel, extents), out_shape=(out, out),...  36.6 us
    unnamed x5, local copies, waits for them, and re-layouts  6.73 us

profile of v1, /device:TPU:0, one launch (start us, length us, event | category | flops | bytes accessed | tf_op | source)
XLA Modules:
  0.0 44.6 jit_solution(10873600297383943883)
XLA Ops:
  1.3 1.3 %copy.16 = s32[1,1,1,3,128]{4,3,2,1,0:T(4,128)} copy(s32[1,1,1,3,128]{4,2,3,1,0:T(1,128)} %param.11) | data formatting | bytes 3072
  2.6 1.3 %copy.15 = f32[1,1,1,6,32]{4,3,2,1,0:T(8,128)} copy(f32[1,1,1,6,32]{4,2,3,1,0:T(1,128)} %param.9) | data formatting | bytes 1536
  3.8 1.3 %copy.14 = f32[1,1,1,6,768]{4,3,2,1,0:T(8,128)} copy(f32[1,1,1,6,768]{4,2,3,1,0:T(1,128)} %param.8) | data formatting | bytes 36864
  5.2 36.6 %shard_map.77 = (f32[32,384]{1,0:T(8,128)}, f32[32,384]{1,0:T(8,128)}) custom-call(bf16[768,768]{1,0:T(8,128)(2,1)} %bitcast.15, f32[32,384]{1,0:T(8,128)} %bitcast.17, f32[6,768]{1,0:T(8,128)} %bitcast.16, f32[6,32]{1,0:T(8,128)} %bitcast.20, s32[1,1]{1,0:T(1,128)} %bitcast.14.count_ref, s32[3,128]{1,0:T(4,128)} %bitcast.21), custom_call_target="tpu_custom_call" | custom-call | tf_op jit(solution)/shard_map/pallas_call | solution.py:459
  41.8 1.4 %copy.20 = f32[1,1,1,32,384]{4,3,2,1,0:T(8,128)} copy(f32[1,1,1,32,384]{4,3,2,1,0:T(8,128)} %bitcast.19) | data formatting | bytes 98304
  43.2 1.4 %copy.21 = f32[1,1,1,32,384]{4,3,2,1,0:T(8,128)} copy(f32[1,1,1,32,384]{4,3,2,1,0:T(8,128)} %bitcast.18) | data formatting | bytes 98304

commit v2 on v1

--- a/solution.py
+++ b/solution.py
@@ -49,14 +49,18 @@
 def kernel(
     extents,
     operator_hbm,
+    load_hbm,
+    modes_hbm,
+    coarse_hbm,
+    count_ref,
+    maps_hbm,
+    multipliers_ref,
+    residual_ref,
+    raw,
     load_ref,
     modes_ref,
     coarse_ref,
-    count_ref,
     maps_ref,
-    multipliers_ref,
-    residual_ref,
-    raw,
     ordered,
     own_modes,
     minus_modes,
@@ -83,17 +87,29 @@
     line_recv,
 ):
     nx, ny, nz = extents
-    cases = load_ref.shape[0]
-    width = load_ref.shape[1] // 3
-    modes = modes_ref.shape[0]
+    cases = load_hbm.shape[0]
+    width = load_hbm.shape[1] // 3
+    modes = modes_hbm.shape[0]
     padded = own_modes.shape[0]
     here = (lax.axis_index("gx"), lax.axis_index("gy"), lax.axis_index("gz"))
     ix, iy, iz = here
     plane = nx * ny
     slot = ix * ny + iy
 
-    fetch = pltpu.make_async_copy(operator_hbm, raw, raw_sem)
-    fetch.start()
+    fetches = [
+        pltpu.make_async_copy(source, target, raw_sem.at[i])
+        for i, (source, target) in enumerate(
+            (
+                (maps_hbm, maps_ref),
+                (modes_hbm, modes_ref),
+                (coarse_hbm, coarse_ref),
+                (load_hbm, load_ref),
+                (operator_hbm, raw),
+            )
+        )
+    ]
+    for fetch in fetches:
+        fetch.start()
 
     for phase in range(3):
         coefficients[phase] = jnp.zeros(coefficients.shape[1:], jnp.float32)
@@ -145,11 +161,14 @@
         pl.when(exists[f])(copy.start)
         waits.append((f, copy))
 
+    for fetch in fetches[:4]:
+        fetch.wait()
     count = count_ref[0, 0]
     lines = lax.broadcasted_iota(jnp.int32, (width, width), 0)
-    orders = [(lines == maps_ref[d : d + 1, :]).astype(jnp.float32) for d in range(3)]
-    own_modes[0:modes, :] = modes_ref[...]
-    padded_load[0:modes, 0:cases] = coarse_ref[...]
+    orders = [(lines == maps_ref[d]).astype(jnp.float32) for d in range(3)]
+    for m in range(modes):
+        own_modes[m : m + 1, :] = modes_ref[m]
+        padded_load[m : m + 1, 0:cases] = coarse_ref[m]
     raw_modes = jnp.where(
         lax.broadcasted_iota(jnp.int32, own_modes.shape, 0) < count, own_modes[...], 0.0
     )
@@ -274,7 +293,7 @@
             ),
         )
 
-    fetch.wait()
+    fetches[4].wait()
     narrow = [order.astype(jnp.bfloat16) for order in orders]
     for d in range(3):
         low = 2 * d * width
@@ -443,6 +462,14 @@
         copy.wait_send()
 
 
+def held(array):
+    return pltpu.with_memory_space_constraint(array, pltpu.HBM)
+
+
+def rows_apart(array):
+    return jnp.swapaxes(array, 2, 3).reshape(array.shape[3], 1, array.shape[4])
+
+
 def local(extents, dual_operators, dual_load, rigid_modes, coarse_load, mode_counts, face_maps):
     size = dual_operators.shape[-1]
     cases = dual_load.shape[-2]
@@ -454,22 +481,27 @@
     tile = 2 * cases // max(1, width // cases)
     f32 = jnp.float32
     vmem = pl.BlockSpec(memory_space=pltpu.VMEM)
+    hbm = pl.BlockSpec(memory_space=pltpu.HBM)
     dma = pltpu.SemaphoreType.DMA
     out = jax.ShapeDtypeStruct((cases, 3 * width), f32)
     multipliers, residual = pl.pallas_call(
         functools.partial(kernel, extents),
         out_shape=(out, out),
         in_specs=[
-            pl.BlockSpec(memory_space=pl.ANY),
-            vmem,
-            vmem,
-            vmem,
+            hbm,
+            hbm,
+            hbm,
+            hbm,
             pl.BlockSpec(memory_space=pltpu.SMEM),
-            vmem,
+            hbm,
         ],
         out_specs=(vmem, vmem),
         scratch_shapes=[
             pltpu.VMEM((size, size), dual_operators.dtype),
+            pltpu.VMEM((cases, 3 * width), f32),
+            pltpu.VMEM((modes, 1, size), f32),
+            pltpu.VMEM((modes, 1, cases), f32),
+            pltpu.VMEM((3, 1, width), jnp.int32),
             pltpu.VMEM((size, size), dual_operators.dtype),
             pltpu.VMEM((padded, size), f32),
             pltpu.VMEM((padded, size), f32),
@@ -481,7 +513,7 @@
             pltpu.VMEM((3, cases, width), f32),
             pltpu.VMEM((2, plane, tile, width), f32),
             pltpu.VMEM((2, nz, tile, width), f32),
-            dma,
+            dma((5,)),
             dma((3, 6)),
             dma((3, 6)),
             dma((3, 6)),
@@ -495,14 +527,15 @@
             dma((2, nz)),
             dma((2, nz)),
         ],
-        compiler_params=pltpu.CompilerParams(collective_id=0, has_side_effects=True),
+        compiler_params=pltpu.CompilerParams(collective_id=0, has_side_effects=True, vmem_limit_bytes=16 * 1024 * 1024
+        ),
     )(
-        dual_operators.reshape(size, size),
-        dual_load.reshape(cases, 3 * width),
-        rigid_modes.reshape(modes, size),
-        coarse_load.reshape(modes, cases),
+        held(dual_operators.reshape(size, size)),
+        held(dual_load.reshape(cases, 3 * width)),
+        held(rows_apart(rigid_modes)),
+        held(rows_apart(coarse_load)),
         mode_counts.reshape(1, 1),
-        face_maps.reshape(3, width),
+        held(rows_apart(face_maps)),
     )
     shape = (1, 1, 1, cases, 3 * width)
     return multipliers.reshape(shape), residual.reshape(shape)

time: 45 us -> 38.7 us (0.86)
  local copies, waits for them, and re-layouts: 6.73 us -> 1.24 us
  Pallas kernels: 36.6 us -> 35.9 us
    unnamed x5 -> x2, local copies, waits for them, and re-layouts: 6.73 us -> 1.24 us
    pallas_call x1, Pallas kernels: 36.6 us -> 35.9 us  [local(): pl.pallas_call(functools.partial(kernel, extents), out_shape=(out, out),...]
where the time goes in v2:
time: 38.7 us; the launch traced here: 38.5 us
  Pallas kernels  35.9 us (93%)
  between operations  1.29 us (3%)
  local copies, waits for them, and re-layouts  1.24 us (3%)
    pallas_call x1, Pallas kernels, local(): pl.pallas_call(functools.partial(kernel, extents), out_shape=(out, out),...  35.9 us
    unnamed x2, local copies, waits for them, and re-layouts  1.24 us

profile of v2, /device:TPU:0, one launch (start us, length us, event | category | flops | bytes accessed | tf_op | source)
XLA Modules:
  0.0 38.5 jit_solution(4566806528137887587)
XLA Ops:
  1.3 35.9 %shard_map.77 = (f32[32,384]{1,0:T(8,128)S(1)}, f32[32,384]{1,0:T(8,128)S(1)}) custom-call(bf16[768,768]{1,0:T(8,128)(2,1)} %bitcast.11, f32[32,384]{1,0:T(8,128)} %bitcast.12, f32[6,1,768]{2,1,0:T(1,128)} %bitcast.13, f32[6,1,32]{2,1,0:T(1,128)} %bitcast.14, s32[1,1]{1,0:T(1,128)} %bitcast.8.count_ref, s32[3,1,128]{2,1,0:T(1,128)} %bitcast.15), custom_call_target="tpu_custom_call" | custom-call | tf_op jit(solution)/shard_map/pallas_call | solution.py:487
  37.2 0.6 %copy.11 = f32[1,1,1,32,384]{4,3,2,1,0:T(8,128)} copy(f32[1,1,1,32,384]{4,3,2,1,0:T(8,128)S(1)} %bitcast.10) | data formatting | bytes 98304
  37.9 0.6 %copy.12 = f32[1,1,1,32,384]{4,3,2,1,0:T(8,128)} copy(f32[1,1,1,32,384]{4,3,2,1,0:T(8,128)S(1)} %bitcast.9) | data formatting | bytes 98304

commit v3 on v2

--- a/solution.py
+++ b/solution.py
@@ -63,22 +63,29 @@
     maps_ref,
     ordered,
     own_modes,
-    minus_modes,
     all_modes,
     padded_load,
-    coefficients,
+    probes,
+    first_out,
+    first_in,
+    pair_out,
+    pair_in,
     face_out,
     face_in,
+    last_out,
+    last_in,
     load_in,
     plane_sums,
     line_sums,
     raw_sem,
-    coefficient_send,
-    coefficient_recv,
+    first_send,
+    first_recv,
     face_send,
     face_recv,
-    mode_send,
-    mode_recv,
+    pair_send,
+    pair_recv,
+    last_send,
+    last_recv,
     load_send,
     load_recv,
     plane_send,
@@ -111,9 +118,13 @@
     for fetch in fetches:
         fetch.start()
 
-    for phase in range(3):
-        coefficients[phase] = jnp.zeros(coefficients.shape[1:], jnp.float32)
     all_modes[...] = jnp.zeros(all_modes.shape, jnp.float32)
+    probes[...] = jnp.zeros(probes.shape, jnp.float32)
+    first_in[...] = jnp.zeros(first_in.shape, jnp.float32)
+    pair_in[...] = jnp.zeros(pair_in.shape, jnp.float32)
+    pair_out[...] = jnp.zeros(pair_out.shape, jnp.float32)
+    face_out[:, :, cases:, :] = jnp.zeros((2, 6, padded, width), jnp.float32)
+    face_in[:, :, cases:, :] = jnp.zeros((2, 6, padded, width), jnp.float32)
     own_modes[...] = jnp.zeros(own_modes.shape, jnp.float32)
     padded_load[...] = jnp.zeros(padded_load.shape, jnp.float32)
 
@@ -123,12 +134,6 @@
 
     def line_peer(offset):
         return (ix, iy, lax.rem(iz + offset, nz))
-
-    barrier = pltpu.get_barrier_semaphore()
-    for offset in range(1, plane):
-        pl.semaphore_signal(barrier, inc=1, device_id=plane_peer(offset), device_id_type=MESH)
-    for offset in range(1, nz):
-        pl.semaphore_signal(barrier, inc=1, device_id=line_peer(offset), device_id_type=MESH)
 
     exists = []
     neighbour = []
@@ -139,13 +144,48 @@
             neighbour.append(tuple(here[a] + (step if a == d else 0) for a in range(3)))
     flags = [jnp.where(e, 1, 0).astype(jnp.int32) for e in exists]
 
+    def moved(position, f):
+        return tuple(position[a] + ((2 * (f % 2) - 1) if a == f // 2 else 0) for a in range(3))
+
+    def both_exist(f, g):
+        if f != g:
+            return jnp.logical_and(exists[f], exists[g])
+        if f % 2:
+            return here[f // 2] < extents[f // 2] - 2
+        return here[f // 2] > 1
+
+    pairs = [
+        (f, g)
+        for f in range(6)
+        for g in range(6)
+        if (f == g or f // 2 < g // 2) and extents[f // 2] > 1 + (f == g) and extents[g // 2] > 1
+    ]
+
+    barrier = pltpu.get_barrier_semaphore()
+    diagonal = 0
+    for f in range(4):
+        for g in range(4, 6):
+            peer = moved(moved(here, f), g)
+
+            @pl.when(both_exist(f, g))
+            def _(peer=peer):
+                pl.semaphore_signal(barrier, inc=1, device_id=peer, device_id_type=MESH)
+
+            diagonal = diagonal + flags[f] * flags[g]
+    for offset in range(1, plane):
+        pl.semaphore_signal(barrier, inc=1, device_id=plane_peer(offset), device_id_type=MESH)
+    for offset in range(1, nz):
+        pl.semaphore_signal(barrier, inc=1, device_id=line_peer(offset), device_id_type=MESH)
+
+
     def face(values, f):
         return values[:, f * width : (f + 1) * width]
 
     def masked(values, f):
         return jnp.where(jnp.full(values.shape, flags[f], jnp.int32) == 1, values, 0.0)
 
-    waits = []
+    sends = [[] for _ in range(6)]
+    pair_sends = [[] for _ in pairs]
 
     def remote(source, target, send, recv, where):
         return pltpu.make_async_remote_copy(
@@ -157,9 +197,13 @@
             device_id_type=MESH,
         )
 
-    def start_to(f, copy):
-        pl.when(exists[f])(copy.start)
-        waits.append((f, copy))
+    def start_to(f, copies):
+        @pl.when(exists[f])
+        def _():
+            for copy in copies:
+                copy.start()
+
+        sends[f].extend(copies)
 
     for fetch in fetches[:4]:
         fetch.wait()
@@ -178,7 +222,6 @@
         pieces.append(masked(face(raw_modes, 2 * d + 1), 2 * d + 1))
     mode_rows = jnp.concatenate(pieces, axis=1)
     own_modes[...] = mode_rows
-    minus_modes[...] = -mode_rows
     all_modes[0:padded, :] = mode_rows
     inactive = lax.broadcasted_iota(jnp.int32, (padded, padded), 0) >= count
     normal = mul(mode_rows, mode_rows, NT) + jnp.where(inactive, identity(padded), 0.0)
@@ -186,70 +229,94 @@
     active_load = jnp.where(
         lax.broadcasted_iota(jnp.int32, padded_load.shape, 0) < count, padded_load[...], 0.0
     )
-    coefficients[0, 0:padded, :] = mul(coarse_inverse, active_load)
-
-    pl.semaphore_wait(barrier, plane - 1 + nz - 1)
-
-    def slot_of(phase, f):
-        return coefficients.at[phase, pl.ds((1 + f) * padded, padded), :]
-
-    def columns(ref, f):
-        return ref.at[:, pl.ds(f * width, width)]
-
-    def send_coefficients(phase):
+    first_part = mul(coarse_inverse, active_load)
+    inverse_modes = mul(coarse_inverse, mode_rows)
+    probes[6 * padded :, :] = inverse_modes
+    for f in range(6):
+        first_out[f, 0:padded, :] = -face(mode_rows, f)
+        first_out[f, padded : 2 * padded, :] = face(inverse_modes, f)
+        first_out[f, 2 * padded :, :] = first_part
+
+    pl.semaphore_wait(barrier, plane - 1 + nz - 1 + diagonal)
+
+    for f in range(6):
+        copies = [
+            remote(first_out.at[f], first_in.at[f ^ 1], first_send.at[f], first_recv.at[f ^ 1], neighbour[f])
+        ]
+        if f % 2:
+            d = f // 2
+            copies.append(
+                remote(
+                    load_ref.at[:, pl.ds(d * width, width)],
+                    load_in.at[d],
+                    load_send.at[d],
+                    load_recv.at[d],
+                    neighbour[f],
+                )
+            )
+        start_to(f, copies)
+
+    def send_round(phase, values, own=None):
+        found = mul(probes[...], values, NT)
+        share = found[6 * padded :] if own is None else own - found[6 * padded :]
+        for f in range(6):
+            face_out[phase, f, 0:cases, :] = face(values, f)
+            face_out[phase, f, cases:, 0:cases] = share
         for f in range(6):
             start_to(
                 f,
-                remote(
-                    coefficients.at[phase, pl.ds(0, padded), :],
-                    slot_of(phase, f ^ 1),
-                    coefficient_send.at[phase, f],
-                    coefficient_recv.at[phase, f ^ 1],
-                    neighbour[f],
-                ),
-            )
-
-    def wait_coefficients(phase):
+                [
+                    remote(
+                        face_out.at[phase, f],
+                        face_in.at[phase, f ^ 1],
+                        face_send.at[phase, f],
+                        face_recv.at[phase, f ^ 1],
+                        neighbour[f],
+                    )
+                ],
+            )
+        for index, (f, g) in enumerate(pairs):
+            pair_out[phase, index, 0:padded, 0:cases] = found[f * padded : (f + 1) * padded]
+            if f != g:
+                pair_out[phase, index, padded:, 0:cases] = found[g * padded : (g + 1) * padded]
+        for index, (f, g) in enumerate(pairs):
+            other = pairs.index((f ^ 1, g ^ 1))
+            copy = remote(
+                pair_out.at[phase, index],
+                pair_in.at[phase, other],
+                pair_send.at[phase, index],
+                pair_recv.at[phase, other],
+                moved(moved(here, f), g),
+            )
+            pl.when(both_exist(f, g))(copy.start)
+            pair_sends[index].append(copy)
+        return found
+
+    def wait_faces(phase, source, target, send, recv):
         for f in range(6):
             copy = remote(
-                coefficients.at[phase, pl.ds(0, padded), :],
-                slot_of(phase, f),
-                coefficient_send.at[phase, f],
-                coefficient_recv.at[phase, f],
-                neighbour[f],
+                source.at[phase, f], target.at[phase, f], send.at[phase, f], recv.at[phase, f], neighbour[f]
             )
             pl.when(exists[f])(copy.wait_recv)
 
-    def coarse_field(phase):
-        return mul(coefficients[phase][:, 0:cases], all_modes[...], TN)
-
-    def send_faces(phase):
-        for f in range(6):
-            start_to(
-                f,
-                remote(
-                    face_out.at[phase, f],
-                    face_in.at[phase, f ^ 1],
-                    face_send.at[phase, f],
-                    face_recv.at[phase, f ^ 1],
-                    neighbour[f],
-                ),
-            )
-
-    def wait_faces(phase):
-        for f in range(6):
+    def wait_pairs(phase):
+        for index, (f, g) in enumerate(pairs):
             copy = remote(
-                face_out.at[phase, f],
-                face_in.at[phase, f],
-                face_send.at[phase, f],
-                face_recv.at[phase, f],
-                neighbour[f],
-            )
-            pl.when(exists[f])(copy.wait_recv)
-
-    def assembled(phase):
+                pair_out.at[phase, index],
+                pair_in.at[phase, index],
+                pair_send.at[phase, index],
+                pair_recv.at[phase, index],
+                moved(moved(here, f), g),
+            )
+            pl.when(both_exist(f, g))(copy.wait_recv)
+
+    def assembled(mine, theirs, phase):
         return jnp.concatenate(
-            [masked(face_out[phase, f] - face_in[phase, f], f) for f in range(6)], axis=1
+            [
+                masked(mine[phase, f, 0:cases, :] - theirs[phase, f, 0:cases, :], f)
+                for f in range(6)
+            ],
+            axis=1,
         )
 
     def apply_local(values):
@@ -262,36 +329,8 @@
         )
         return both[0:cases] + both[cases:]
 
-    def keep_faces(phase, values):
-        for f in range(6):
-            face_out[phase, f] = face(values, f)
-
     def owned(values):
         return jnp.concatenate([face(values, 1), face(values, 3), face(values, 5)], axis=1)
-
-    for f in range(6):
-        start_to(
-            f,
-            remote(
-                columns(minus_modes, f),
-                all_modes.at[pl.ds((1 + (f ^ 1)) * padded, padded), pl.ds((f ^ 1) * width, width)],
-                mode_send.at[f],
-                mode_recv.at[f ^ 1],
-                neighbour[f],
-            ),
-        )
-    send_coefficients(0)
-    for d in range(3):
-        start_to(
-            2 * d + 1,
-            remote(
-                columns(load_ref, d),
-                load_in.at[d],
-                load_send.at[d],
-                load_recv.at[d],
-                neighbour[2 * d + 1],
-            ),
-        )
 
     fetches[4].wait()
     narrow = [order.astype(jnp.bfloat16) for order in orders]
@@ -306,46 +345,51 @@
             raw[:, low : low + width], narrow[d], NT, preferred_element_type=jnp.float32
         ).astype(jnp.bfloat16)
         ordered[:, low + width : low + 2 * width] = raw[:, low + width : low + 2 * width]
-    inverse_modes = mul(coarse_inverse, mode_rows)
-
     for f in range(6):
-        copy = remote(
-            columns(minus_modes, f),
-            all_modes.at[pl.ds((1 + f) * padded, padded), pl.ds(f * width, width)],
-            mode_send.at[f],
-            mode_recv.at[f],
-            neighbour[f],
-        )
-        pl.when(exists[f])(copy.wait_recv)
-    wait_coefficients(0)
-    initial = coarse_field(0)
+        d = f // 2
+        first = remote(first_out.at[f], first_in.at[f], first_send.at[f], first_recv.at[f], neighbour[f])
+        pl.when(exists[f])(first.wait_recv)
+    coefficients = [first_part]
+    for f in range(6):
+        all_modes[(1 + f) * padded : (2 + f) * padded, f * width : (f + 1) * width] = first_in[
+            f, 0:padded, :
+        ]
+        probes[f * padded : (f + 1) * padded, f * width : (f + 1) * width] = first_in[
+            f, padded : 2 * padded, :
+        ]
+        coefficients.append(first_in[f, 2 * padded :, :])
+    initial = mul(jnp.concatenate(coefficients, axis=0)[:, 0:cases], all_modes[...], TN)
     product = apply_local(initial)
-    keep_faces(0, product)
-    send_faces(0)
+    right = []
     for d in range(3):
         copy = remote(
-            columns(load_ref, d),
+            load_ref.at[:, pl.ds(d * width, width)],
             load_in.at[d],
             load_send.at[d],
             load_recv.at[d],
             neighbour[2 * d],
         )
         pl.when(exists[2 * d])(copy.wait_recv)
-    right = []
     for d in range(3):
         right.append(masked(-load_in[d], 2 * d))
         right.append(masked(load_ref[:, d * width : (d + 1) * width], 2 * d + 1))
     right = jnp.concatenate(right, axis=1)
-    wait_faces(0)
-    residual = right - assembled(0)
-
-    def precondition(phase, values):
-        coefficients[phase, 0:padded, 0:cases] = mul(inverse_modes, values, NT)
-        send_coefficients(phase)
-
-    def preconditioned(phase, values):
-        wait_coefficients(phase)
-        return values - 0.25 * coarse_field(phase)
+    found = send_round(0, product, mul(inverse_modes, right, NT))
+    wait_faces(0, face_out, face_in, face_send, face_recv)
+    residual = right - assembled(face_out, face_in, 0)
+
+    def preconditioned(phase, values, found, sign):
+        own = mul(inverse_modes, values, NT)
+        wait_pairs(phase)
+        terms = [found[f * padded : (f + 1) * padded] for f in range(6)]
+        for index, (a, b) in enumerate(pairs):
+            terms[b] = terms[b] + pair_in[phase, index, 0:padded, 0:cases]
+            if a != b:
+                terms[a] = terms[a] + pair_in[phase, index, padded:, 0:cases]
+        every = [own]
+        for f in range(6):
+            every.append(face_in[phase, f, cases:, 0:cases] - sign * terms[f])
+        return values - 0.25 * mul(jnp.concatenate(every, axis=0), all_modes[...], TN)
 
     def sum_start(which, tile):
         plane_sums[which, slot] = tile
@@ -403,11 +447,9 @@
         half = total.shape[0] // 2
         return unpacked(total[0:half], cases), unpacked(total[half:], cases)
 
-    precondition(1, residual)
-    start = preconditioned(1, residual)
+    start = preconditioned(0, residual, found, -1.0)
     product = apply_local(start)
-    keep_faces(1, product)
-    send_faces(1)
+    found = send_round(1, product)
     early = sum_start(
         0,
         jnp.concatenate(
@@ -418,13 +460,11 @@
             axis=0,
         ),
     )
-    wait_faces(1)
-    image = assembled(1)
-    precondition(2, image)
+    wait_faces(1, face_out, face_in, face_send, face_recv)
+    image = assembled(face_out, face_in, 1)
+    second = preconditioned(1, image, found, 1.0)
     sum_middle(0, early)
-    second = preconditioned(2, image)
     product = apply_local(second)
-    keep_faces(2, product)
     late = sum_start(
         1,
         jnp.concatenate(
@@ -435,13 +475,27 @@
             axis=0,
         ),
     )
-    send_faces(2)
+    for f in range(6):
+        last_out[0, f] = face(product, f)
+    for f in range(6):
+        start_to(
+            f,
+            [
+                remote(
+                    last_out.at[0, f],
+                    last_in.at[0, f ^ 1],
+                    last_send.at[0, f],
+                    last_recv.at[0, f ^ 1],
+                    neighbour[f],
+                )
+            ],
+        )
     gram, energy = sum_end(0)
     inverse = eliminate(jnp.concatenate([energy, identity(cases)], axis=1), cases)
     alpha = mul(inverse, gram)
     sum_middle(1, late)
-    wait_faces(2)
-    second_image = assembled(2)
+    wait_faces(0, last_out, last_in, last_send, last_recv)
+    second_image = assembled(last_out, last_in, 0)
     cross, last = sum_end(1)
     carried = mul(inverse, cross)
     schur = last - mul(cross, carried)
@@ -456,8 +510,16 @@
         both, jnp.concatenate([owned(image), owned(second_image)], axis=0), TN
     )
 
-    for f, copy in waits:
-        pl.when(exists[f])(copy.wait_send)
+    def finish(condition, copies):
+        @pl.when(condition)
+        def _():
+            for copy in copies:
+                copy.wait_send()
+
+    for f in range(6):
+        finish(exists[f], sends[f])
+    for index, (f, g) in enumerate(pairs):
+        finish(both_exist(f, g), pair_sends[index])
     for copy in early + late:
         copy.wait_send()
 
@@ -504,22 +566,29 @@
             pltpu.VMEM((3, 1, width), jnp.int32),
             pltpu.VMEM((size, size), dual_operators.dtype),
             pltpu.VMEM((padded, size), f32),
-            pltpu.VMEM((padded, size), f32),
             pltpu.VMEM((7 * padded, size), f32),
             pltpu.VMEM((padded, width), f32),
-            pltpu.VMEM((3, 7 * padded, width), f32),
-            pltpu.VMEM((3, 6, cases, width), f32),
-            pltpu.VMEM((3, 6, cases, width), f32),
+            pltpu.VMEM((7 * padded, size), f32),
+            pltpu.VMEM((6, 3 * padded, width), f32),
+            pltpu.VMEM((6, 3 * padded, width), f32),
+            pltpu.VMEM((2, 18, 2 * padded, width), f32),
+            pltpu.VMEM((2, 18, 2 * padded, width), f32),
+            pltpu.VMEM((2, 6, cases + padded, width), f32),
+            pltpu.VMEM((2, 6, cases + padded, width), f32),
+            pltpu.VMEM((1, 6, cases, width), f32),
+            pltpu.VMEM((1, 6, cases, width), f32),
             pltpu.VMEM((3, cases, width), f32),
             pltpu.VMEM((2, plane, tile, width), f32),
             pltpu.VMEM((2, nz, tile, width), f32),
             dma((5,)),
-            dma((3, 6)),
-            dma((3, 6)),
-            dma((3, 6)),
-            dma((3, 6)),
             dma((6,)),
             dma((6,)),
+            dma((2, 6)),
+            dma((2, 6)),
+            dma((2, 18)),
+            dma((2, 18)),
+            dma((1, 6)),
+            dma((1, 6)),
             dma((3,)),
             dma((3,)),
             dma((2, plane)),

time: 38.7 us -> 37.2 us (0.961)
  Pallas kernels: 35.9 us -> 34.5 us
    pallas_call x1, Pallas kernels: 35.9 us -> 34.5 us  [local(): pl.pallas_call(functools.partial(kernel, extents), out_shape=(out, out),...]
where the time goes in v3:
time: 37.2 us; the launch traced here: 37 us
  Pallas kernels  34.5 us (93%)
  between operations  1.29 us (3%)
  local copies, waits for them, and re-layouts  1.24 us (3%)
    pallas_call x1, Pallas kernels, local(): pl.pallas_call(functools.partial(kernel, extents), out_shape=(out, out),...  34.5 us
    unnamed x2, local copies, waits for them, and re-layouts  1.24 us

profile of v3, /device:TPU:0, one launch (start us, length us, event | category | flops | bytes accessed | tf_op | source)
XLA Modules:
  0.0 37.0 jit_solution(13612398109994013985)
XLA Ops:
  1.3 34.5 %shard_map.77 = (f32[32,384]{1,0:T(8,128)S(1)}, f32[32,384]{1,0:T(8,128)S(1)}) custom-call(bf16[768,768]{1,0:T(8,128)(2,1)} %bitcast.11, f32[32,384]{1,0:T(8,128)} %bitcast.12, f32[6,1,768]{2,1,0:T(1,128)} %bitcast.13, f32[6,1,32]{2,1,0:T(1,128)} %bitcast.14, s32[1,1]{1,0:T(1,128)} %bitcast.8.count_ref, s32[3,1,128]{2,1,0:T(1,128)} %bitcast.15), custom_call_target="tpu_custom_call" | custom-call | tf_op jit(solution)/shard_map/pallas_call | solution.py:549
  35.8 0.6 %copy.11 = f32[1,1,1,32,384]{4,3,2,1,0:T(8,128)} copy(f32[1,1,1,32,384]{4,3,2,1,0:T(8,128)S(1)} %bitcast.10) | data formatting | bytes 98304
  36.4 0.6 %copy.12 = f32[1,1,1,32,384]{4,3,2,1,0:T(8,128)} copy(f32[1,1,1,32,384]{4,3,2,1,0:T(8,128)S(1)} %bitcast.9) | data formatting | bytes 98304

commit v4 on v3

--- a/solution.py
+++ b/solution.py
@@ -18,13 +18,46 @@
     return lax.dot_general(a, b, dims, precision=HIGH, preferred_element_type=jnp.float32)
 
 
-def eliminate(system, size):
+def split(a):
+    head = a.astype(jnp.bfloat16)
+    return head, (a - head.astype(jnp.float32)).astype(jnp.bfloat16)
+
+
+def fast(a, b, dims=NN):
+    if dims == TN:
+        a, dims = a.T, NN
+    (ah, al), (bh, bl) = split(a), split(b)
+    dot = functools.partial(
+        lax.dot_general, dimension_numbers=dims, preferred_element_type=jnp.float32
+    )
+    return dot(ah, bh) + (dot(ah, bl) + dot(al, bh))
+
+
+def eliminate(system, size, block=4):
     rows = lax.broadcasted_iota(jnp.int32, system.shape, 0)
-    for k in range(size):
-        row = system[k : k + 1, :]
-        column = system[:, k : k + 1]
-        scaled = row / row[:, k : k + 1]
-        system = jnp.where(rows == k, scaled, system - column * scaled)
+    span = range(block)
+    for k in range(0, size, block):
+        columns = [system[:, k + j : k + j + 1] for j in span]
+        lines = [system[k + i : k + i + 1, :] for i in span]
+        pivots = [
+            [jnp.broadcast_to(lines[i][:, k + j : k + j + 1], lines[i].shape) for j in span]
+            for i in span
+        ]
+        for j in span:
+            scale = 1.0 / pivots[j][j]
+            lines[j] = lines[j] * scale
+            pivots[j] = [p * scale for p in pivots[j]]
+            for i in span:
+                if i != j:
+                    factor = pivots[i][j]
+                    lines[i] = lines[i] - factor * lines[j]
+                    pivots[i] = [p - factor * q for p, q in zip(pivots[i], pivots[j])]
+        update = columns[0] * lines[0]
+        for j in span[1:]:
+            update = update + columns[j] * lines[j]
+        system = system - update
+        for j in span:
+            system = jnp.where(rows == k + j, lines[j], system)
     return system[:, size:]
 
 
@@ -123,8 +156,8 @@
     first_in[...] = jnp.zeros(first_in.shape, jnp.float32)
     pair_in[...] = jnp.zeros(pair_in.shape, jnp.float32)
     pair_out[...] = jnp.zeros(pair_out.shape, jnp.float32)
-    face_out[:, :, cases:, :] = jnp.zeros((2, 6, padded, width), jnp.float32)
-    face_in[:, :, cases:, :] = jnp.zeros((2, 6, padded, width), jnp.float32)
+    face_out[:, :, cases:, :] = jnp.zeros((2, 6, 2 * padded, width), jnp.float32)
+    face_in[:, :, cases:, :] = jnp.zeros((2, 6, 2 * padded, width), jnp.float32)
     own_modes[...] = jnp.zeros(own_modes.shape, jnp.float32)
     padded_load[...] = jnp.zeros(padded_load.shape, jnp.float32)
 
@@ -257,11 +290,27 @@
         start_to(f, copies)
 
     def send_round(phase, values, own=None):
-        found = mul(probes[...], values, NT)
+        found = fast(probes[...], values, NT)
         share = found[6 * padded :] if own is None else own - found[6 * padded :]
         for f in range(6):
             face_out[phase, f, 0:cases, :] = face(values, f)
-            face_out[phase, f, cases:, 0:cases] = share
+            face_out[phase, f, cases : cases + padded, 0:cases] = share
+            face_out[phase, f, cases + padded :, 0:cases] = found[f * padded : (f + 1) * padded]
+        for index, (f, g) in enumerate(pairs):
+            pair_out[phase, index, 0:padded, 0:cases] = found[f * padded : (f + 1) * padded]
+            if f != g:
+                pair_out[phase, index, padded:, 0:cases] = found[g * padded : (g + 1) * padded]
+        for index, (f, g) in enumerate(pairs):
+            other = pairs.index((f ^ 1, g ^ 1))
+            copy = remote(
+                pair_out.at[phase, index],
+                pair_in.at[phase, other],
+                pair_send.at[phase, index],
+                pair_recv.at[phase, other],
+                moved(moved(here, f), g),
+            )
+            pl.when(both_exist(f, g))(copy.start)
+            pair_sends[index].append(copy)
         for f in range(6):
             start_to(
                 f,
@@ -275,22 +324,7 @@
                     )
                 ],
             )
-        for index, (f, g) in enumerate(pairs):
-            pair_out[phase, index, 0:padded, 0:cases] = found[f * padded : (f + 1) * padded]
-            if f != g:
-                pair_out[phase, index, padded:, 0:cases] = found[g * padded : (g + 1) * padded]
-        for index, (f, g) in enumerate(pairs):
-            other = pairs.index((f ^ 1, g ^ 1))
-            copy = remote(
-                pair_out.at[phase, index],
-                pair_in.at[phase, other],
-                pair_send.at[phase, index],
-                pair_recv.at[phase, other],
-                moved(moved(here, f), g),
-            )
-            pl.when(both_exist(f, g))(copy.start)
-            pair_sends[index].append(copy)
-        return found
+        return found, share
 
     def wait_faces(phase, source, target, send, recv):
         for f in range(6):
@@ -358,7 +392,7 @@
             f, padded : 2 * padded, :
         ]
         coefficients.append(first_in[f, 2 * padded :, :])
-    initial = mul(jnp.concatenate(coefficients, axis=0)[:, 0:cases], all_modes[...], TN)
+    initial = fast(jnp.concatenate(coefficients, axis=0)[:, 0:cases], all_modes[...], TN)
     product = apply_local(initial)
     right = []
     for d in range(3):
@@ -374,12 +408,16 @@
         right.append(masked(-load_in[d], 2 * d))
         right.append(masked(load_ref[:, d * width : (d + 1) * width], 2 * d + 1))
     right = jnp.concatenate(right, axis=1)
-    found = send_round(0, product, mul(inverse_modes, right, NT))
+    shares = send_round(0, product, fast(inverse_modes, right, NT))
     wait_faces(0, face_out, face_in, face_send, face_recv)
     residual = right - assembled(face_out, face_in, 0)
 
-    def preconditioned(phase, values, found, sign):
-        own = mul(inverse_modes, values, NT)
+    def preconditioned(phase, values, shares, sign):
+        found, own = shares
+        back = face_in[phase, 0, cases + padded :, 0:cases]
+        for f in range(1, 6):
+            back = back + face_in[phase, f, cases + padded :, 0:cases]
+        own = own - sign * back
         wait_pairs(phase)
         terms = [found[f * padded : (f + 1) * padded] for f in range(6)]
         for index, (a, b) in enumerate(pairs):
@@ -388,8 +426,8 @@
                 terms[a] = terms[a] + pair_in[phase, index, padded:, 0:cases]
         every = [own]
         for f in range(6):
-            every.append(face_in[phase, f, cases:, 0:cases] - sign * terms[f])
-        return values - 0.25 * mul(jnp.concatenate(every, axis=0), all_modes[...], TN)
+            every.append(face_in[phase, f, cases : cases + padded, 0:cases] - sign * terms[f])
+        return values - 0.25 * fast(jnp.concatenate(every, axis=0), all_modes[...], TN)
 
     def sum_start(which, tile):
         plane_sums[which, slot] = tile
@@ -447,30 +485,30 @@
         half = total.shape[0] // 2
         return unpacked(total[0:half], cases), unpacked(total[half:], cases)
 
-    start = preconditioned(0, residual, found, -1.0)
+    start = preconditioned(0, residual, shares, -1.0)
     product = apply_local(start)
-    found = send_round(1, product)
+    shares = send_round(1, product)
     early = sum_start(
         0,
         jnp.concatenate(
             [
-                packed(mul(owned(start), owned(residual), NT), width),
-                packed(mul(start, product, NT), width),
+                packed(fast(owned(start), owned(residual), NT), width),
+                packed(fast(start, product, NT), width),
             ],
             axis=0,
         ),
     )
     wait_faces(1, face_out, face_in, face_send, face_recv)
     image = assembled(face_out, face_in, 1)
-    second = preconditioned(1, image, found, 1.0)
     sum_middle(0, early)
+    second = preconditioned(1, image, shares, 1.0)
     product = apply_local(second)
     late = sum_start(
         1,
         jnp.concatenate(
             [
-                packed(mul(owned(second), owned(image), NT), width),
-                packed(mul(second, product, NT), width),
+                packed(fast(owned(second), owned(image), NT), width),
+                packed(fast(second, product, NT), width),
             ],
             axis=0,
         ),
@@ -492,21 +530,21 @@
         )
     gram, energy = sum_end(0)
     inverse = eliminate(jnp.concatenate([energy, identity(cases)], axis=1), cases)
-    alpha = mul(inverse, gram)
+    alpha = fast(inverse, gram)
     sum_middle(1, late)
     wait_faces(0, last_out, last_in, last_send, last_recv)
     second_image = assembled(last_out, last_in, 0)
     cross, last = sum_end(1)
-    carried = mul(inverse, cross)
-    schur = last - mul(cross, carried)
-    right_side = mul(cross, alpha) - energy
+    carried = fast(inverse, cross)
+    schur = last - fast(cross, carried)
+    right_side = fast(cross, alpha) - energy
     tail = eliminate(jnp.concatenate([schur, right_side], axis=1), cases)
-    head = alpha + mul(carried, tail)
+    head = alpha + fast(carried, tail)
     both = jnp.concatenate([head, -tail], axis=0)
-    multipliers_ref[...] = owned(initial) + mul(
+    multipliers_ref[...] = owned(initial) + fast(
         both, jnp.concatenate([owned(start), owned(second)], axis=0), TN
     )
-    residual_ref[...] = owned(residual) - mul(
+    residual_ref[...] = owned(residual) - fast(
         both, jnp.concatenate([owned(image), owned(second_image)], axis=0), TN
     )
 
@@ -573,8 +611,8 @@
             pltpu.VMEM((6, 3 * padded, width), f32),
             pltpu.VMEM((2, 18, 2 * padded, width), f32),
             pltpu.VMEM((2, 18, 2 * padded, width), f32),
-            pltpu.VMEM((2, 6, cases + padded, width), f32),
-            pltpu.VMEM((2, 6, cases + padded, width), f32),
+            pltpu.VMEM((2, 6, cases + 2 * padded, width), f32),
+            pltpu.VMEM((2, 6, cases + 2 * padded, width), f32),
             pltpu.VMEM((1, 6, cases, width), f32),
             pltpu.VMEM((1, 6, cases, width), f32),
             pltpu.VMEM((3, cases, width), f32),

time: 37.2 us -> 33.5 us (0.901)
  Pallas kernels: 34.5 us -> 30.8 us
    pallas_call x1, Pallas kernels: 34.5 us -> 30.8 us  [local(): pl.pallas_call(functools.partial(kernel, extents), out_shape=(out, out),...]
where the time goes in v4:
time: 33.5 us; the launch traced here: 33.4 us
  Pallas kernels  30.8 us (92%)
  between operations  1.29 us (4%)
  local copies, waits for them, and re-layouts  1.24 us (4%)
    pallas_call x1, Pallas kernels, local(): pl.pallas_call(functools.partial(kernel, extents), out_shape=(out, out),...  30.8 us
    unnamed x2, local copies, waits for them, and re-layouts  1.24 us

profile of v4, /device:TPU:0, one launch (start us, length us, event | category | flops | bytes accessed | tf_op | source)
XLA Modules:
  0.0 33.4 jit_solution(8072912520931147011)
XLA Ops:
  1.3 30.8 %shard_map.77 = (f32[32,384]{1,0:T(8,128)S(1)}, f32[32,384]{1,0:T(8,128)S(1)}) custom-call(bf16[768,768]{1,0:T(8,128)(2,1)} %bitcast.11, f32[32,384]{1,0:T(8,128)} %bitcast.12, f32[6,1,768]{2,1,0:T(1,128)} %bitcast.13, f32[6,1,32]{2,1,0:T(1,128)} %bitcast.14, s32[1,1]{1,0:T(1,128)} %bitcast.8.count_ref, s32[3,1,128]{2,1,0:T(1,128)} %bitcast.15), custom_call_target="tpu_custom_call" | custom-call | tf_op jit(solution)/shard_map/pallas_call | solution.py:587
  32.1 0.6 %copy.11 = f32[1,1,1,32,384]{4,3,2,1,0:T(8,128)} copy(f32[1,1,1,32,384]{4,3,2,1,0:T(8,128)S(1)} %bitcast.10) | data formatting | bytes 98304
  32.7 0.6 %copy.12 = f32[1,1,1,32,384]{4,3,2,1,0:T(8,128)} copy(f32[1,1,1,32,384]{4,3,2,1,0:T(8,128)S(1)} %bitcast.9) | data formatting | bytes 98304

commit v5 on v4

--- a/solution.py
+++ b/solution.py
@@ -33,7 +33,7 @@
     return dot(ah, bh) + (dot(ah, bl) + dot(al, bh))
 
 
-def eliminate(system, size, block=4):
+def eliminate(system, size, block=8):
     rows = lax.broadcasted_iota(jnp.int32, system.shape, 0)
     span = range(block)
     for k in range(0, size, block):

time: 33.5 us -> 33 us (0.985)
  Pallas kernels: 30.8 us -> 30.3 us
    pallas_call x1, Pallas kernels: 30.8 us -> 30.3 us  [local(): pl.pallas_call(functools.partial(kernel, extents), out_shape=(out, out),...]
where the time goes in v5:
time: 33 us; the launch traced here: 32.8 us
  Pallas kernels  30.3 us (92%)
  between operations  1.29 us (4%)
  local copies, waits for them, and re-layouts  1.24 us (4%)
    pallas_call x1, Pallas kernels, local(): pl.pallas_call(functools.partial(kernel, extents), out_shape=(out, out),...  30.3 us
    unnamed x2, local copies, waits for them, and re-layouts  1.24 us

profile of v5, /device:TPU:0, one launch (start us, length us, event | category | flops | bytes accessed | tf_op | source)
XLA Modules:
  0.0 32.8 jit_solution(17473142532335491969)
XLA Ops:
  1.3 30.3 %shard_map.77 = (f32[32,384]{1,0:T(8,128)S(1)}, f32[32,384]{1,0:T(8,128)S(1)}) custom-call(bf16[768,768]{1,0:T(8,128)(2,1)} %bitcast.11, f32[32,384]{1,0:T(8,128)} %bitcast.12, f32[6,1,768]{2,1,0:T(1,128)} %bitcast.13, f32[6,1,32]{2,1,0:T(1,128)} %bitcast.14, s32[1,1]{1,0:T(1,128)} %bitcast.8.count_ref, s32[3,1,128]{2,1,0:T(1,128)} %bitcast.15), custom_call_target="tpu_custom_call" | custom-call | tf_op jit(solution)/shard_map/pallas_call | solution.py:587
  31.6 0.6 %copy.11 = f32[1,1,1,32,384]{4,3,2,1,0:T(8,128)} copy(f32[1,1,1,32,384]{4,3,2,1,0:T(8,128)S(1)} %bitcast.10) | data formatting | bytes 98304
  32.2 0.6 %copy.12 = f32[1,1,1,32,384]{4,3,2,1,0:T(8,128)} copy(f32[1,1,1,32,384]{4,3,2,1,0:T(8,128)S(1)} %bitcast.9) | data formatting | bytes 98304
